TPU v7x, 32 devices: a whole 2x2x4 slice. The times are simulated.
32 devices in a mesh: vocab: 8 (over z, y), dp: 4 (over x, core).
Axes of the slice: x: 2, y: 2, z: 4, core: 2. Of those that a mesh axis runs over, the one named last changes fastest.
Arguments:
- hidden: bfloat16 [2, 128, 7168], P(None, ('vocab', 'dp')), may hold values from -18 to 18
- unembed: bfloat16 [7168, 8192], P(None, ('vocab', 'dp')), may hold values from -0.24803919 to 0.24803919
- targets: int32 [2, 128], replicated, may hold values from 0 to 8191
Outputs:
- token_loss: float32 [2, 128], P(None, ('vocab', 'dp'))
- total_loss: float32 [], replicated
All inputs are finite; a program needn't handle non-finite values.
Results may differ from a plain program's by a relative error of at most 0.0003.
Values may be sent and summed in bfloat16 or wider, within the bound.
No kernel may reach another device: no remote copies, remote signals or barrier semaphores. Data moves between devices by JAX's collectives and lax.ppermute only.
A program may use at most 128 MiB of HBM per device.

v0:
```python
import jax
import jax.numpy as jnp
from jax import lax
from jax.sharding import PartitionSpec as P

MTP_WEIGHT = 0.3


def partner(value, axis, apart):
    mask = 2**apart
    pairs = [(source, source ^ mask) for source in range(lax.axis_size(axis))]
    return lax.ppermute(value, axis, pairs)


def block_stats(row_block, columns, first_column, wanted):
    logits = jnp.einsum("srd,dc->src", row_block, columns, preferred_element_type=jnp.float32)
    highest = jnp.max(logits, axis=2)
    exp_total = jnp.sum(jnp.exp(logits - highest[:, :, None]), axis=2)
    column_ids = first_column + lax.broadcasted_iota(jnp.int32, logits.shape, 2)
    picked = jnp.sum(jnp.where(column_ids == wanted[:, :, None], logits, 0.0), axis=2)
    return (highest, exp_total, picked)


def join_stats(earlier, later):
    highest = jnp.maximum(earlier[0], later[0])
    exp_total = earlier[1] * jnp.exp(earlier[0] - highest) + later[1] * jnp.exp(later[0] - highest)
    return (highest, exp_total, earlier[2] + later[2])


def reduce_sources(received, source_dims):
    highest = jnp.max(received[0], axis=source_dims)
    expanded = jnp.expand_dims(highest, source_dims)
    exp_total = jnp.sum(received[1] * jnp.exp(received[0] - expanded), axis=source_dims)
    picked = jnp.sum(received[2], axis=source_dims)
    return (highest, exp_total, picked)


def finish(partial_sums):
    return partial_sums[0] + jnp.log(partial_sums[1]) - partial_sums[2]


def local(hidden, unembed, targets):
    tok_rows = hidden.shape[1]
    column_width = unembed.shape[1]
    n_vocab = lax.axis_size("vocab")
    n_data = lax.axis_size("dp")
    token_count = tok_rows * n_vocab * n_data
    vocab_index = lax.axis_index("vocab")
    data_index = lax.axis_index("dp")
    joined_index = vocab_index * n_data + data_index
    bit_count = n_data.bit_length() - 1
    low_bit = data_index % 2
    gathered = lax.all_gather(hidden, "vocab", axis=1, tiled=True)
    token_block = gathered[:, None]
    for bit_number in range(1, bit_count):
        other = partner(token_block, "dp", bit_number)
        is_upper = data_index // 2**bit_number % 2 == 1
        lower_half = jnp.where(is_upper, other, token_block)
        upper_half = jnp.where(is_upper, token_block, other)
        token_block = jnp.concatenate([lower_half, upper_half], axis=1)
    group_count = token_block.shape[1]
    row_block = token_block.reshape(2, group_count * n_vocab * tok_rows, token_block.shape[3])
    arranged = targets.reshape(2, n_vocab, group_count, 2, tok_rows)
    picked_targets = lax.dynamic_index_in_dim(arranged, low_bit, 3, keepdims=False)
    wanted = jnp.transpose(picked_targets, (0, 2, 1, 3)).reshape(
        2, group_count * n_vocab * tok_rows
    )
    partner_columns = partner(unembed, "dp", 0)
    own_first = joined_index * column_width
    partner_first = (vocab_index * n_data + data_index + 1 - 2 * low_bit) * column_width
    own_stats = block_stats(row_block, unembed, own_first, wanted)
    partner_stats = block_stats(row_block, partner_columns, partner_first, wanted)
    partial_sums = join_stats(own_stats, partner_stats)
    shaped = tuple((member.reshape(2, group_count, n_vocab, tok_rows) for member in partial_sums))
    received = lax.all_to_all(shaped, "vocab", split_axis=2, concat_axis=2, tiled=True)
    current = reduce_sources(received, (2,))
    for bit_number in range(bit_count - 1, 0, -1):
        half_count = current[0].shape[1] // 2
        is_upper = data_index // 2**bit_number % 2 == 1
        halves = tuple((member.reshape(2, 2, half_count, tok_rows) for member in current))
        keeping = tuple((jnp.where(is_upper, member[:, 1], member[:, 0]) for member in halves))
        sending = tuple((jnp.where(is_upper, member[:, 0], member[:, 1]) for member in halves))
        arrived = partner(sending, "dp", bit_number)
        current = join_stats(keeping, arrived)
    token_loss = finish(tuple((member.reshape(2, tok_rows) for member in current)))
    loss_sums = lax.psum((jnp.sum(token_loss[0]), jnp.sum(token_loss[1])), ("vocab", "dp"))
    total_loss = loss_sums[0] / token_count + MTP_WEIGHT * loss_sums[1] / token_count
    return (token_loss, total_loss)


def solution(mesh):
    placed = (P(None, ("vocab", "dp"), None), P(None, ("vocab", "dp")), P())
    return jax.shard_map(
        local,
        mesh=mesh,
        in_specs=placed,
        out_specs=(P(None, ("vocab", "dp")), P()),
        check_vma=False,
    )
```

profile of v0, /device:TPU:0, one launch (start us, length us, event | category | flops | bytes accessed | tf_op | source)
XLA Modules:
  0.0 142.3 jit_solution(14423498156459414771)
XLA Ops:
  0.6 1.0 copy.11
  1.6 34.2 %all_gather.3 = bf16[2,32,7168]{2,0,1:T(2,128)(2,1)S(1)} all-gather(bf16[2,4,7168]{2,0,1:T(2,128)(2,1)S(1)} %copy.11), channel_id=1, replica_groups=mesh['vocab'=8,'dp'=4] {'vocab'}, dimensions={1}, use_global_device_ids=true | all-gather | bytes 1032192 | tf_op jit(solution)/shard_map/all_gather | solution.py:53
  35.9 1.5 %collective-permute-start = (bf16[2,1,32,7168]{3,0,2,1:T(2,128)(2,1)S(1)}, bf16[2,1,32,7168]{3,0,2,1:T(2,128)(2,1)S(1)}, u32[]{:S(2)}, u32[]{:S(2)}) collective-permute-start(bf16[2,1,32,7168]{3,0,2,1:T(2,128)(2,1)S(1)} %bitcast.33), channel_id=1, source_target_pairs={{0,2},{1,3},{2,0},{3,1},{4,6},{5,7},{6,4},{7,5},{8,10},{9,11},{10,... | collective-permute-start | bytes 2752520 | tf_op jit(solution)/shard_map/ppermute | solution.py:12
  37.4 0.0 collective-permute-start.1
  37.4 0.8 reshape.178
  38.2 0.1 copy.15
  38.3 0.1 copy.16
  38.4 0.1 eq.25
  38.5 14.0 %collective-permute-done = bf16[2,1,32,7168]{3,0,2,1:T(2,128)(2,1)S(1)} collective-permute-done((bf16[2,1,32,7168]{3,0,2,1:T(2,128)(2,1)S(1)}, bf16[2,1,32,7168]{3,0,2,1:T(2,128)(2,1)S(1)}, u32[]{:S(2)}, u32[]{:S(2)}) %collective-permute-start) | collective-permute-done | bytes 917536 | tf_op jit(solution)/shard_map/ppermute | solution.py:12
  52.5 1.4 broadcast_select_fusion.1
  53.9 2.6 %pad_maximum_fusion = bf16[2,2,32,7168]{3,0,2,1:T(2,128)(2,1)S(1)} fusion(bf16[2,1,32,7168]{3,0,2,1:T(2,128)(2,1)S(1)} %get-tuple-element.13, bf16[2,1,32,7168]{3,0,2,1:T(2,128)(2,1)S(1)} %get-tuple-element.12), kind=kLoop, calls=%fused_computation.4 | loop fusion | flops 917504 | bytes 3670016 | tf_op jit(solution)/shard_map/concatenate | solution.py:60
  56.5 0.0 copy-start
  56.5 0.4 copy.12
  56.9 1.7 %copy-done = bf16[7168,256]{1,0:T(8,128)(2,1)S(1)} copy-done((bf16[7168,256]{1,0:T(8,128)(2,1)S(1)}, bf16[7168,256]{1,0:T(8,128)(2,1)}, u32[]{:S(2)}) %copy-start) | copy-done | bytes 3670040
  58.6 0.8 fusion.7
  59.4 0.1 reduce_max.32
  59.5 0.0 collective-permute-done.1
  59.5 2.8 %fusion.6 = (f32[2,64]{1,0:T(2,128)S(1)}, f32[2,64,256]{2,1,0:T(8,128)S(1)}) fusion(bf16[2,64,7168]{2,1,0:T(8,128)(2,1)S(1)} %bitcast.32, bf16[7168,256]{1,0:T(8,128)(2,1)} %collective-permute-done.1), kind=kOutput, calls=%fused_computation.28 | convolution fusion | flops 469794688 | bytes 5636608 | tf_op jit(solution)/shard_map/srd,dc->src/dot_general | solution.py:16
  62.2 0.1 reduce_max.34
  62.3 0.3 exponential_reduce_fusion
  62.6 0.1 reduce_sum.77
  62.7 0.1 reduce_sum.79
  62.8 0.6 copy.13
  63.4 5.3 %all-to-all-start = ((f32[2,2,8,4]{3,1,0,2:T(2,128)}), f32[2,2,8,4]{3,1,0,2:T(2,128)S(1)}, u32[]{:S(2)}, u32[]{:S(2)}) async-start(f32[2,2,8,4]{3,1,0,2:T(2,128)} %copy.13), calls=%async_computation | async-start | bytes 32768 | tf_op jit(solution)/shard_map/all_to_all | solution.py:75
  68.7 0.6 copy.14
  69.3 6.0 %all-to-all-done = f32[2,2,8,4]{3,1,0,2:T(2,128)S(1)} async-done(((f32[2,2,8,4]{3,1,0,2:T(2,128)}), f32[2,2,8,4]{3,1,0,2:T(2,128)S(1)}, u32[]{:S(2)}, u32[]{:S(2)}) %all-to-all-start) | async-done | bytes 544 | tf_op jit(solution)/shard_map/all_to_all | solution.py:75
  75.3 3.3 %all-to-all-start.1 = ((f32[2,2,8,4]{3,1,0,2:T(2,128)}), f32[2,2,8,4]{3,1,0,2:T(2,128)S(1)}, u32[]{:S(2)}, u32[]{:S(2)}) async-start(f32[2,2,8,4]{3,1,0,2:T(2,128)} %copy.14), calls=%async_computation.1 | async-start | bytes 32768 | tf_op jit(solution)/shard_map/all_to_all | solution.py:75
  78.6 0.1 add.75
  78.7 0.6 copy.17
  79.3 5.8 %all-to-all-done.1 = f32[2,2,8,4]{3,1,0,2:T(2,128)S(1)} async-done(((f32[2,2,8,4]{3,1,0,2:T(2,128)}), f32[2,2,8,4]{3,1,0,2:T(2,128)S(1)}, u32[]{:S(2)}, u32[]{:S(2)}) %all-to-all-start.1) | async-done | bytes 544 | tf_op jit(solution)/shard_map/all_to_all | solution.py:75
  85.1 3.3 %all-to-all-start.2 = ((f32[2,2,8,4]{3,1,0,2:T(2,128)}), f32[2,2,8,4]{3,1,0,2:T(2,128)S(1)}, u32[]{:S(2)}, u32[]{:S(2)}) async-start(f32[2,2,8,4]{3,1,0,2:T(2,128)} %copy.17), calls=%async_computation.2 | async-start | bytes 32768 | tf_op jit(solution)/shard_map/all_to_all | solution.py:75
  88.5 6.5 %all-to-all-done.2 = f32[2,2,8,4]{3,1,0,2:T(2,128)S(1)} async-done(((f32[2,2,8,4]{3,1,0,2:T(2,128)}), f32[2,2,8,4]{3,1,0,2:T(2,128)S(1)}, u32[]{:S(2)}, u32[]{:S(2)}) %all-to-all-start.2) | async-done | bytes 544 | tf_op jit(solution)/shard_map/all_to_all | solution.py:75
  95.0 1.6 %collective-permute-start.3 = (f32[2,1,4]{2,0,1:T(2,128)S(1)}, f32[2,1,4]{2,0,1:T(2,128)S(1)}, u32[]{:S(2)}, u32[]{:S(2)}) collective-permute-start(f32[2,1,4]{2,0,1:T(2,128)S(1)} %bitcast.43), channel_id=1, source_target_pairs={{0,2},{1,3},{2,0},{3,1},{4,6},{5,7},{6,4},{7,5},{8,10},{9,11},{10,... | collective-permute-start | bytes 104 | tf_op jit(solution)/shard_map/ppermute | solution.py:12
  96.6 0.5 collective-permute-start.4
  97.1 1.5 %collective-permute-start.2 = (f32[2,1,4]{2,0,1:T(2,128)S(1)}, f32[2,1,4]{2,0,1:T(2,128)S(1)}, u32[]{:S(2)}, u32[]{:S(2)}) collective-permute-start(f32[2,1,4]{2,0,1:T(2,128)S(1)} %bitcast.44), channel_id=1, source_target_pairs={{0,2},{1,3},{2,0},{3,1},{4,6},{5,7},{6,4},{7,5},{8,10},{9,11},{10,... | collective-permute-start | bytes 104 | tf_op jit(solution)/shard_map/ppermute | solution.py:12
  98.6 0.1 collective-permute-done.3
  98.6 1.5 %collective-permute-done.4 = f32[2,1,4]{2,0,1:T(2,128)S(1)} collective-permute-done((f32[2,1,4]{2,0,1:T(2,128)S(1)}, f32[2,1,4]{2,0,1:T(2,128)S(1)}, u32[]{:S(2)}, u32[]{:S(2)}) %collective-permute-start.4) | collective-permute-done | bytes 64 | tf_op jit(solution)/shard_map/ppermute | solution.py:12
  100.1 0.5 collective-permute-done.2
  100.7 0.0 copy-start.1
  100.7 0.7 slice_reduce_fusion
  101.4 38.5 %all-reduce = (f32[]{:T(128)}, f32[]{:T(128)}) all-reduce(f32[]{:T(128)} %get-tuple-element.7, f32[]{:T(128)} %get-tuple-element.6), channel_id=1, replica_groups=mesh['vocab'=8,'dp'=4] {'vocab','dp'}, use_global_device_ids=true, to_apply=%region_10.11 | all-reduce | flops 2 | bytes 16 | tf_op jit(solution)/shard_map/psum | solution.py:86
  141.1 0.0 copy-done.1
  (11 shorter events, 0.2 us)
Async XLA Ops:
  35.9 16.6 %collective-permute-start = (bf16[2,1,32,7168]{3,0,2,1:T(2,128)(2,1)S(1)}, bf16[2,1,32,7168]{3,0,2,1:T(2,128)(2,1)S(1)}, u32[]{:S(2)}, u32[]{:S(2)}) collective-permute-start(bf16[2,1,32,7168]{3,0,2,1:T(2,128)(2,1)S(1)} %bitcast.33), channel_id=1, source_target_pairs={{0,2},{1,3},{2,0},{3,1},{4,6},{5,7},{6,4},{7,5},{8,10},{9,11},{10,... | collective-permute-start | bytes 2752520 | tf_op jit(solution)/shard_map/ppermute | solution.py:12
  37.4 22.1 %collective-permute-start.1 = (bf16[7168,256]{1,0:T(8,128)(2,1)}, bf16[7168,256]{1,0:T(8,128)(2,1)}, u32[]{:S(2)}, u32[]{:S(2)}) collective-permute-start(bf16[7168,256]{1,0:T(8,128)(2,1)} %param.4), channel_id=1, source_target_pairs={{0,1},{1,0},{2,3},{3,2},{4,5},{5,4},{6,7},{7,6},{8,9},{9,8},{10,11... | collective-permute-start | bytes 11010056 | tf_op jit(solution)/shard_map/ppermute | solution.py:12
  56.5 2.0 %copy-start = (bf16[7168,256]{1,0:T(8,128)(2,1)S(1)}, bf16[7168,256]{1,0:T(8,128)(2,1)}, u32[]{:S(2)}) copy-start(bf16[7168,256]{1,0:T(8,128)(2,1)} %param.4) | copy-start | bytes 11010052
  63.4 11.8 %all-to-all-start = ((f32[2,2,8,4]{3,1,0,2:T(2,128)}), f32[2,2,8,4]{3,1,0,2:T(2,128)S(1)}, u32[]{:S(2)}, u32[]{:S(2)}) async-start(f32[2,2,8,4]{3,1,0,2:T(2,128)} %copy.13), calls=%async_computation | async-start | bytes 32768 | tf_op jit(solution)/shard_map/all_to_all | solution.py:75
  75.3 9.9 %all-to-all-start.1 = ((f32[2,2,8,4]{3,1,0,2:T(2,128)}), f32[2,2,8,4]{3,1,0,2:T(2,128)S(1)}, u32[]{:S(2)}, u32[]{:S(2)}) async-start(f32[2,2,8,4]{3,1,0,2:T(2,128)} %copy.14), calls=%async_computation.1 | async-start | bytes 32768 | tf_op jit(solution)/shard_map/all_to_all | solution.py:75
  85.1 9.8 %all-to-all-start.2 = ((f32[2,2,8,4]{3,1,0,2:T(2,128)}), f32[2,2,8,4]{3,1,0,2:T(2,128)S(1)}, u32[]{:S(2)}, u32[]{:S(2)}) async-start(f32[2,2,8,4]{3,1,0,2:T(2,128)} %copy.17), calls=%async_computation.2 | async-start | bytes 32768 | tf_op jit(solution)/shard_map/all_to_all | solution.py:75
  95.0 3.6 %collective-permute-start.3 = (f32[2,1,4]{2,0,1:T(2,128)S(1)}, f32[2,1,4]{2,0,1:T(2,128)S(1)}, u32[]{:S(2)}, u32[]{:S(2)}) collective-permute-start(f32[2,1,4]{2,0,1:T(2,128)S(1)} %bitcast.43), channel_id=1, source_target_pairs={{0,2},{1,3},{2,0},{3,1},{4,6},{5,7},{6,4},{7,5},{8,10},{9,11},{10,... | collective-permute-start | bytes 104 | tf_op jit(solution)/shard_map/ppermute | solution.py:12
  96.6 3.6 %collective-permute-start.4 = (f32[2,1,4]{2,0,1:T(2,128)S(1)}, f32[2,1,4]{2,0,1:T(2,128)S(1)}, u32[]{:S(2)}, u32[]{:S(2)}) collective-permute-start(f32[2,1,4]{2,0,1:T(2,128)S(1)} %bitcast.42), channel_id=1, source_target_pairs={{0,2},{1,3},{2,0},{3,1},{4,6},{5,7},{6,4},{7,5},{8,10},{9,11},{10,... | collective-permute-start | bytes 104 | tf_op jit(solution)/shard_map/ppermute | solution.py:12
  97.1 3.6 %collective-permute-start.2 = (f32[2,1,4]{2,0,1:T(2,128)S(1)}, f32[2,1,4]{2,0,1:T(2,128)S(1)}, u32[]{:S(2)}, u32[]{:S(2)}) collective-permute-start(f32[2,1,4]{2,0,1:T(2,128)S(1)} %bitcast.44), channel_id=1, source_target_pairs={{0,2},{1,3},{2,0},{3,1},{4,6},{5,7},{6,4},{7,5},{8,10},{9,11},{10,... | collective-permute-start | bytes 104 | tf_op jit(solution)/shard_map/ppermute | solution.py:12
  100.7 40.4 %copy-start.1 = (f32[2,1,4]{2,0,1:T(2,128)}, f32[2,1,4]{2,0,1:T(2,128)S(1)}, u32[]{:S(2)}) copy-start(f32[2,1,4]{2,0,1:T(2,128)S(1)} %add_subtract_fusion) | copy-start | bytes 100
where the time goes:
time: 143 us; the launch traced here: 142 us
  blocking collectives  72.8 us (51%)
  waiting for transfers between devices  34.3 us (24%)
  starting transfers between devices  17 us (12%)
  local copies, waits for them, and re-layouts  6.37 us (4%)
  other arithmetic  5.13 us (4%)
  matrix products  3.57 us (2%)
  between operations  3.13 us (2%)
    psum x1, blocking collectives, local(): lax.psum((jnp.sum(token_loss[0]), jnp.sum(token_loss[1])), ('vocab', 'dp'))  38.5 us
    all_gather x1, blocking collectives, local(): gathered = lax.all_gather(hidden, 'vocab', axis=1, tiled=True)  34.2 us
    all_to_all x3, waiting for transfers between devices, local(): lax.all_to_all(shaped, 'vocab', split_axis=2, concat_axis=2, tiled=True)  18.2 us
    ppermute x5, waiting for transfers between devices, partner(): return lax.ppermute(value, axis, pairs)  16.1 us
    all_to_all x3, starting transfers between devices, local(): lax.all_to_all(shaped, 'vocab', split_axis=2, concat_axis=2, tiled=True)  11.9 us
    ppermute x5, starting transfers between devices, partner(): return lax.ppermute(value, axis, pairs)  5.08 us
    dot_general x2, matrix products, block_stats(): jnp.einsum('srd,dc->src', row_block, columns, preferred_element_type=jnp....  3.57 us
  transfers between devices with their start and end apart: 8, of which 7 were waited for; matrix products, arithmetic and copies ran while one was open for 5% of the time, Pallas kernels for 0%

commit v1 on v0

v1 whole, which is shorter than its diff:
```python
import functools
import jax
import jax.numpy as jnp
from jax import lax
from jax.experimental import pallas as pl
from jax.experimental.pallas import tpu as pltpu
from jax.sharding import Mesh, PartitionSpec as P

MTP_WEIGHT = 0.3
AXES = ("vocab", "chip", "core")
CHIPS = ("vocab", "chip")


def bits(count):
    return [1 << place for place in range(count.bit_length() - 1)]


def gather_orders(n_vocab, n_chip):
    near = bits(n_chip) + [n_chip * mask for mask in bits(n_vocab)[:1]]
    far = [n_chip * mask for mask in bits(n_vocab)[1:]]
    return (far[::-1] + near, far + near[::-1])


def exchange(value, masks, n_chips):
    pairs = [(2 * chip + core, 2 * (chip ^ masks[core]) + core) for chip in range(n_chips) for core in range(2)]
    return lax.ppermute(value, AXES, pairs)


def to_other_core(value, n_chips):
    pairs = [(source, source ^ 1) for source in range(2 * n_chips)]
    return lax.ppermute(value, AXES, pairs)


def offset(masks, place):
    total = 0
    for number, mask in enumerate(masks):
        if place >> number & 1:
            total ^= mask
    return total


def stats_kernel(orders, block, n_chip, wanted, kept, arrived, own, other, out, logits):
    core = lax.axis_index("core")
    chip = lax.axis_index("vocab") * n_chip + lax.axis_index("chip")
    width = own.shape[1]
    blocks = kept.shape[0] // block
    for part, rows in enumerate((kept, arrived)):
        for side, columns in enumerate((own, other)):
            product = jnp.dot(rows[...], columns[...], preferred_element_type=jnp.float32)
            for number in range(blocks):
                place = part * blocks + number
                shift = jnp.where(core == 0, offset(orders[0], place), offset(orders[1], place))
                first = pl.multiple_of((chip ^ shift) * block, block)
                logits[pl.ds(first, block), pl.ds(side * width, width)] = product[number * block : (number + 1) * block]
    values = logits[...]
    highest = jnp.max(values, axis=1, keepdims=True)
    exp_total = jnp.sum(jnp.exp(values - highest), axis=1, keepdims=True)
    device = 2 * chip + core
    lane = lax.broadcasted_iota(jnp.int32, values.shape, 1)
    column_ids = jnp.where(lane < width, device * width + lane, (device ^ 1) * width + lane - width)
    picked = jnp.sum(jnp.where(column_ids == wanted[...], values, 0.0), axis=1, keepdims=True)
    member = lax.broadcasted_iota(jnp.int32, (values.shape[0], 128), 1)
    table = jnp.where(member == 0, highest, jnp.where(member == 1, exp_total, picked))
    sent = jnp.transpose(table)[:8]
    for chip_number in range(out.shape[0]):
        out[chip_number] = sent


def loss_kernel(n_chip, block, heads_rows, received, own_loss, part):
    chip = lax.axis_index("vocab") * n_chip + lax.axis_index("chip")
    rows = received.shape[2]
    highs = received[:, 0, :]
    highest = jnp.max(highs, axis=0, keepdims=True)
    exp_total = jnp.sum(received[:, 1, :] * jnp.exp(highs - highest), axis=0, keepdims=True)
    picked = jnp.sum(received[:, 2, :], axis=0, keepdims=True)
    loss = highest + jnp.log(exp_total) - picked
    lane = lax.broadcasted_iota(jnp.int32, loss.shape, 1)
    weight = jnp.where(lane // heads_rows % 2 == 0, 1.0 / rows, MTP_WEIGHT / rows)
    part[...] = jnp.broadcast_to(jnp.sum(loss * weight, axis=1, keepdims=True), part.shape)
    turned = pltpu.roll(jnp.broadcast_to(loss, (8, rows)), rows - chip * block, 1)
    own_loss[...] = turned[:, :128]


def local(hidden, unembed, targets):
    heads, tok_rows, depth = hidden.shape
    block = heads * tok_rows
    width = unembed.shape[1]
    n_vocab, n_chip = lax.axis_size("vocab"), lax.axis_size("chip")
    n_chips = n_vocab * n_chip
    orders = gather_orders(n_vocab, n_chip)
    core = lax.axis_index("core")
    rows = n_chips * block

    other_columns = to_other_core(unembed, n_chips)
    kept = hidden.reshape(block, depth)
    for number in range(len(orders[0])):
        arrived = exchange(kept, (orders[0][number], orders[1][number]), n_chips)
        if number < len(orders[0]) - 1:
            kept = jnp.concatenate([kept, arrived], axis=0)
    mine = lax.dynamic_index_in_dim(targets.reshape(heads, n_chips, 2, tok_rows), core, 2, keepdims=False)
    wanted = jnp.transpose(mine, (1, 0, 2)).reshape(rows, 1)
    held = 2 * (rows + 2 * width) * depth + 4 * rows * (4 * width + 2 * 128 + 8 * n_chips)
    sent = pl.pallas_call(
        functools.partial(stats_kernel, orders, block, n_chip),
        out_shape=jax.ShapeDtypeStruct((n_chips, 8, rows), jnp.float32),
        scratch_shapes=[pltpu.VMEM((rows, 2 * width), jnp.float32)],
        cost_estimate=pl.CostEstimate(flops=4 * rows * width * depth, bytes_accessed=4 * (rows + width) * depth, transcendentals=0),
        compiler_params=pltpu.CompilerParams(vmem_limit_bytes=held + 2**21),
        name="stats",
    )(wanted, kept, arrived, unembed, other_columns)
    received = lax.all_to_all(sent, CHIPS, split_axis=0, concat_axis=0, tiled=True)
    own_loss, part = pl.pallas_call(
        functools.partial(loss_kernel, n_chip, block, tok_rows),
        out_shape=(jax.ShapeDtypeStruct((8, 128), jnp.float32), jax.ShapeDtypeStruct((8, 128), jnp.float32)),
        compiler_params=pltpu.CompilerParams(vmem_limit_bytes=2**20 + 4 * 4 * n_chips * 8 * rows),
        name="loss",
    )(received)
    token_loss = own_loss[0, :block].reshape(heads, tok_rows)
    total = part[0, 0] + to_other_core(part, n_chips)[0, 0]
    return token_loss, total


def solution(mesh):
    n_vocab, n_data = mesh.shape["vocab"], mesh.shape["dp"]
    fine = Mesh(mesh.devices.reshape(n_vocab, n_data // 2, 2), AXES)
    return jax.shard_map(
        local,
        mesh=fine,
        in_specs=(P(None, AXES, None), P(None, AXES), P()),
        out_specs=(P(None, AXES), P()),
        check_vma=False,
    )
```

time: 143 us -> 65.9 us (0.46)
  blocking collectives: 72.8 us -> 16.1 us
  waiting for transfers between devices: 34.3 us -> 25.3 us
  starting transfers between devices: 17 us -> 10.2 us
  other arithmetic: 5.13 us -> 0.05 us
  Pallas kernels: 0 us -> 5.02 us
  matrix products: 3.57 us -> 0 us
    psum x1 -> x0, blocking collectives: 38.5 us -> none  [local(): lax.psum((jnp.sum(token_loss[0]), jnp.sum(token_loss[1])), ('vocab', 'dp'))]
    all_gather x1 -> x0, blocking collectives: 34.2 us -> none  [local(): gathered = lax.all_gather(hidden, 'vocab', axis=1, tiled=True)]
    all_to_all x3 -> x0, waiting for transfers between devices: 18.2 us -> none  [local(): lax.all_to_all(shaped, 'vocab', split_axis=2, concat_axis=2, tiled=True)]
    all_to_all x0 -> x1, blocking collectives: none -> 16.1 us  [local(): lax.all_to_all(sent, CHIPS, split_axis=0, concat_axis=0, tiled=True)]
    all_to_all x3 -> x0, starting transfers between devices: 11.9 us -> none  [local(): lax.all_to_all(shaped, 'vocab', split_axis=2, concat_axis=2, tiled=True)]
    ppermute x5 -> x6, waiting for transfers between devices: 16.1 us -> 25.3 us  [the longest x4 25.3 us: exchange(): return lax.ppermute(value, AXES, pairs)]
    ppermute x5 -> x6, starting transfers between devices: 5.08 us -> 10.2 us  [the longest x4 10.2 us: exchange(): return lax.ppermute(value, AXES, pairs)]
    pallas_call x0 -> x2, Pallas kernels: none -> 5.02 us  [the longest x1 4.92 us: local(): pl.pallas_call(functools.partial(stats_kernel, orders, block, n_chip), ou...]
  transfers between devices with their start and end apart: 8 -> 6, of which waited for: 7 -> 4; matrix products, arithmetic and copies ran while one was open for 5% -> 4% of each run, Pallas kernels for 0% -> 0%
where the time goes in v1:
time: 65.9 us; the launch traced here: 65.6 us
  waiting for transfers between devices  25.3 us (38%)
  blocking collectives  16.1 us (24%)
  starting transfers between devices  10.2 us (15%)
  local copies, waits for them, and re-layouts  5.8 us (9%)
  Pallas kernels  5.02 us (8%)
  between operations  3.03 us (5%)
    ppermute x4, waiting for transfers between devices, exchange(): return lax.ppermute(value, AXES, pairs)  25.3 us
    all_to_all x1, blocking collectives, local(): lax.all_to_all(sent, CHIPS, split_axis=0, concat_axis=0, tiled=True)  16.1 us
    ppermute x4, starting transfers between devices, exchange(): return lax.ppermute(value, AXES, pairs)  10.2 us
    pallas_call x1, Pallas kernels, local(): pl.pallas_call(functools.partial(stats_kernel, orders, block, n_chip), ou...  4.92 us
    unnamed x5, local copies, waits for them, and re-layouts  2.07 us
  transfers between devices with their start and end apart: 6, of which 4 were waited for; matrix products, arithmetic and copies ran while one was open for 4% of the time, Pallas kernels for 0%

profile of v1, /device:TPU:0, one launch (start us, length us, event | category | flops | bytes accessed | tf_op | source)
XLA Modules:
  0.0 65.6 jit_solution(17261821847242413304)
XLA Ops:
  0.6 0.9 %reshape.16 = bf16[8,7168]{1,0:T(8,128)(2,1)S(1)} reshape(bf16[2,4,7168]{2,1,0:T(4,128)(2,1)} %param.3) | data formatting | bytes 229376 | tf_op jit(solution)/shard_map/reshape | solution.py:95
  1.6 4.1 %collective-permute-start = (bf16[8,7168]{1,0:T(8,128)(2,1)S(1)}, bf16[8,7168]{1,0:T(8,128)(2,1)S(1)}, u32[]{:S(2)}, u32[]{:S(2)}) collective-permute-start(bf16[8,7168]{1,0:T(8,128)(2,1)S(1)} %reshape.16), channel_id=1, source_target_pairs={{0,16},{1,9},{2,18},{3,11},{4,20},{5,13},{6,22},{7,15},{8,24},{9,1... | collective-permute-start | bytes 344072 | tf_op jit(solution)/shard_map/ppermute | solution.py:26
  5.7 0.0 collective-permute-start.4
  5.7 2.8 %collective-permute-done = bf16[8,7168]{1,0:T(8,128)(2,1)S(1)} collective-permute-done((bf16[8,7168]{1,0:T(8,128)(2,1)S(1)}, bf16[8,7168]{1,0:T(8,128)(2,1)S(1)}, u32[]{:S(2)}, u32[]{:S(2)}) %collective-permute-start) | collective-permute-done | bytes 114720 | tf_op jit(solution)/shard_map/ppermute | solution.py:26
  8.5 2.3 %collective-permute-start.1 = (bf16[16,7168]{1,0:T(8,128)(2,1)S(1)}, bf16[16,7168]{1,0:T(8,128)(2,1)S(1)}, u32[]{:S(2)}, u32[]{:S(2)}) collective-permute-start(bf16[16,7168]{1,0:T(8,128)(2,1)S(1)} %pad_maximum_fusion.1), channel_id=1, source_target_pairs={{0,8},{1,17},{2,10},{3,19},{4,12},{5,21},{6,14},{7,23},{8,0},{9,25... | collective-permute-start | bytes 688136 | tf_op jit(solution)/shard_map/ppermute | solution.py:26
  10.8 5.5 %collective-permute-done.1 = bf16[16,7168]{1,0:T(8,128)(2,1)S(1)} collective-permute-done((bf16[16,7168]{1,0:T(8,128)(2,1)S(1)}, bf16[16,7168]{1,0:T(8,128)(2,1)S(1)}, u32[]{:S(2)}, u32[]{:S(2)}) %collective-permute-start.1) | collective-permute-done | bytes 229408 | tf_op jit(solution)/shard_map/ppermute | solution.py:26
  16.3 1.9 %collective-permute-start.2 = (bf16[32,7168]{1,0:T(8,128)(2,1)S(1)}, bf16[32,7168]{1,0:T(8,128)(2,1)S(1)}, u32[]{:S(2)}, u32[]{:S(2)}) collective-permute-start(bf16[32,7168]{1,0:T(8,128)(2,1)S(1)} %pad_maximum_fusion), channel_id=1, source_target_pairs={{0,2},{1,5},{2,0},{3,7},{4,6},{5,1},{6,4},{7,3},{8,10},{9,13},{10,... | collective-permute-start | bytes 1376264 | tf_op jit(solution)/shard_map/ppermute | solution.py:26
  18.2 6.6 %collective-permute-done.2 = bf16[32,7168]{1,0:T(8,128)(2,1)S(1)} collective-permute-done((bf16[32,7168]{1,0:T(8,128)(2,1)S(1)}, bf16[32,7168]{1,0:T(8,128)(2,1)S(1)}, u32[]{:S(2)}, u32[]{:S(2)}) %collective-permute-start.2) | collective-permute-done | bytes 458784 | tf_op jit(solution)/shard_map/ppermute | solution.py:26
  24.9 1.9 %collective-permute-start.3 = (bf16[64,7168]{1,0:T(8,128)(2,1)S(1)}, bf16[64,7168]{1,0:T(8,128)(2,1)S(1)}, u32[]{:S(2)}, u32[]{:S(2)}) collective-permute-start(bf16[64,7168]{1,0:T(8,128)(2,1)S(1)} %constant_dynamic-update-slice_fusion.kept), channel_id=1, source_target_pairs={{0,4},{1,3},{2,6},{3,1},{4,0},{5,7},{6,2},{7,5},{8,12},{9,11},{10,... | collective-permute-start | bytes 2752520 | tf_op jit(solution)/shard_map/ppermute | solution.py:26
  26.8 0.8 %reshape.14 = s32[2,16,2,4]{3,2,1,0:T(2,128)S(1)} reshape(s32[2,128]{1,0:T(2,128)} %param.5) | data formatting | bytes 2048 | tf_op jit(solution)/shard_map/reshape | solution.py:100
  27.6 0.1 copy.8
  27.7 0.1 copy.9
  27.8 0.1 reshape.17.wanted
  27.9 10.4 %collective-permute-done.3.arrived = bf16[64,7168]{1,0:T(8,128)(2,1)S(1)} collective-permute-done((bf16[64,7168]{1,0:T(8,128)(2,1)S(1)}, bf16[64,7168]{1,0:T(8,128)(2,1)S(1)}, u32[]{:S(2)}, u32[]{:S(2)}) %collective-permute-start.3) | collective-permute-done | bytes 917536 | tf_op jit(solution)/shard_map/ppermute | solution.py:26
  38.4 0.0 collective-permute-done.4.other
  38.4 0.0 copy-start
  38.4 2.0 %copy-done = bf16[7168,256]{1,0:T(8,128)(2,1)S(1)} copy-done((bf16[7168,256]{1,0:T(8,128)(2,1)S(1)}, bf16[7168,256]{1,0:T(8,128)(2,1)}, u32[]{:S(2)}) %copy-start) | copy-done | bytes 3670040
  40.4 4.9 %stats.1 = f32[16,8,128]{2,1,0:T(8,128)S(1)} custom-call(s32[128,1]{1,0:T(8,128)S(1)} %reshape.17.wanted, bf16[64,7168]{1,0:T(8,128)(2,1)S(1)} %constant_dynamic-update-slice_fusion.kept, bf16[64,7168]{1,0:T(8,128)(2,1)S(1)} %collective-permute-done.3.arrived, bf16[7168,256]{1,0:T(8,128)(2,1)S(1)} %copy-done, bf16[7168,256]{1,0:T(8,128)(2,1)} %collective-permute-done.4.other), custom_call_target="tpu_custom_call" | custom-call | flops 939524096 | bytes 11010048 | tf_op jit(solution)/shard_map/stats/pallas_call | solution.py:103
  45.3 16.1 %all_to_all.5.received = f32[16,8,128]{2,1,0:T(8,128)S(1)} all-to-all(f32[16,8,128]{2,1,0:T(8,128)S(1)} %stats.1), channel_id=1, replica_groups=mesh['vocab'=8,'chip'=2,'core'=2] {'vocab','chip'}, dimensions={0} | all-to-all | bytes 131072 | tf_op jit(solution)/shard_map/all_to_all | solution.py:111
  61.5 0.1 loss.1
  61.6 0.0 collective-permute-start.5
  61.6 0.5 slice.10
  62.1 0.6 reshape_squeeze.3
  62.8 0.0 collective-permute-done.5
  62.8 0.5 slice.11
  (8 shorter events, 0.1 us)
Async XLA Ops:
  1.6 6.9 %collective-permute-start = (bf16[8,7168]{1,0:T(8,128)(2,1)S(1)}, bf16[8,7168]{1,0:T(8,128)(2,1)S(1)}, u32[]{:S(2)}, u32[]{:S(2)}) collective-permute-start(bf16[8,7168]{1,0:T(8,128)(2,1)S(1)} %reshape.16), channel_id=1, source_target_pairs={{0,16},{1,9},{2,18},{3,11},{4,20},{5,13},{6,22},{7,15},{8,24},{9,1... | collective-permute-start | bytes 344072 | tf_op jit(solution)/shard_map/ppermute | solution.py:26
  5.7 32.7 %collective-permute-start.4 = (bf16[7168,256]{1,0:T(8,128)(2,1)}, bf16[7168,256]{1,0:T(8,128)(2,1)}, u32[]{:S(2)}, u32[]{:S(2)}) collective-permute-start(bf16[7168,256]{1,0:T(8,128)(2,1)} %own.1), channel_id=1, source_target_pairs={{0,1},{1,0},{2,3},{3,2},{4,5},{5,4},{6,7},{7,6},{8,9},{9,8},{10,11... | collective-permute-start | bytes 11010056 | tf_op jit(solution)/shard_map/ppermute | solution.py:31
  8.5 7.8 %collective-permute-start.1 = (bf16[16,7168]{1,0:T(8,128)(2,1)S(1)}, bf16[16,7168]{1,0:T(8,128)(2,1)S(1)}, u32[]{:S(2)}, u32[]{:S(2)}) collective-permute-start(bf16[16,7168]{1,0:T(8,128)(2,1)S(1)} %pad_maximum_fusion.1), channel_id=1, source_target_pairs={{0,8},{1,17},{2,10},{3,19},{4,12},{5,21},{6,14},{7,23},{8,0},{9,25... | collective-permute-start | bytes 688136 | tf_op jit(solution)/shard_map/ppermute | solution.py:26
  16.3 8.5 %collective-permute-start.2 = (bf16[32,7168]{1,0:T(8,128)(2,1)S(1)}, bf16[32,7168]{1,0:T(8,128)(2,1)S(1)}, u32[]{:S(2)}, u32[]{:S(2)}) collective-permute-start(bf16[32,7168]{1,0:T(8,128)(2,1)S(1)} %pad_maximum_fusion), channel_id=1, source_target_pairs={{0,2},{1,5},{2,0},{3,7},{4,6},{5,1},{6,4},{7,3},{8,10},{9,13},{10,... | collective-permute-start | bytes 1376264 | tf_op jit(solution)/shard_map/ppermute | solution.py:26
  24.9 13.5 %collective-permute-start.3 = (bf16[64,7168]{1,0:T(8,128)(2,1)S(1)}, bf16[64,7168]{1,0:T(8,128)(2,1)S(1)}, u32[]{:S(2)}, u32[]{:S(2)}) collective-permute-start(bf16[64,7168]{1,0:T(8,128)(2,1)S(1)} %constant_dynamic-update-slice_fusion.kept), channel_id=1, source_target_pairs={{0,4},{1,3},{2,6},{3,1},{4,0},{5,7},{6,2},{7,5},{8,12},{9,11},{10,... | collective-permute-start | bytes 2752520 | tf_op jit(solution)/shard_map/ppermute | solution.py:26
  38.4 2.0 %copy-start = (bf16[7168,256]{1,0:T(8,128)(2,1)S(1)}, bf16[7168,256]{1,0:T(8,128)(2,1)}, u32[]{:S(2)}) copy-start(bf16[7168,256]{1,0:T(8,128)(2,1)} %own.1) | copy-start | bytes 11010052
  61.6 1.2 %collective-permute-start.5 = (f32[8,128]{1,0:T(8,128)S(1)}, f32[8,128]{1,0:T(8,128)S(1)}, u32[]{:S(2)}, u32[]{:S(2)}) collective-permute-start(f32[8,128]{1,0:T(8,128)S(1)} %get-tuple-element.5), channel_id=1, source_target_pairs={{0,1},{1,0},{2,3},{3,2},{4,5},{5,4},{6,7},{7,6},{8,9},{9,8},{10,11... | collective-permute-start | bytes 12296 | tf_op jit(solution)/shard_map/ppermute | solution.py:31

commit v2 on v1

--- a/solution.py
+++ b/solution.py
@@ -18,7 +18,10 @@
 def gather_orders(n_vocab, n_chip):
     near = bits(n_chip) + [n_chip * mask for mask in bits(n_vocab)[:1]]
     far = [n_chip * mask for mask in bits(n_vocab)[1:]]
-    return (far[::-1] + near, far + near[::-1])
+    return (
+        (far[::-1] + near, far + near[::-1]),
+        (near + far[::-1], near[::-1] + far),
+    )
 
 
 def exchange(value, masks, n_chips):
@@ -39,19 +42,46 @@
     return total
 
 
-def stats_kernel(orders, block, n_chip, wanted, kept, arrived, own, other, out, logits):
+def add_products(orders, block, part, n_chip, rows, columns, first_depth, logits):
+    core = lax.axis_index("core")
+    chip = lax.axis_index("vocab") * n_chip + lax.axis_index("chip")
+    blocks = rows.shape[0] // block
+    depth = pl.ds(first_depth, rows.shape[1])
+    for side, column in enumerate(columns):
+        width = column.shape[1]
+        product = jnp.dot(rows[...], column[depth, :], preferred_element_type=jnp.float32)
+        for number in range(blocks):
+            place = part * blocks + number
+            shift = jnp.where(core == 0, offset(orders[0], place), offset(orders[1], place))
+            first = pl.multiple_of((chip ^ shift) * block, block)
+            target = (pl.ds(first, block), pl.ds(side * width, width))
+            logits[target] = logits[target] + product[number * block : (number + 1) * block]
+
+
+def kept_kernel(flows, block, n_chip, kept_a, kept_b, own, other, own_out, other_out, logits, arrivals):
+    cut, depth = kept_a.shape[1], own.shape[0]
+    pieces = ((0, cut), (cut, depth - cut))
+    copies = []
+    for number, (first, count) in enumerate(pieces):
+        for side, (source, target) in enumerate(((own, own_out), (other, other_out))):
+            span = pl.ds(first, count)
+            copies.append(pltpu.make_async_copy(source.at[span], target.at[span], arrivals.at[2 * number + side]))
+    for copy in copies:
+        copy.start()
+    logits[...] = jnp.zeros_like(logits)
+    for number, kept in enumerate((kept_a, kept_b)):
+        copies[2 * number].wait()
+        copies[2 * number + 1].wait()
+        add_products(flows[number], block, 0, n_chip, kept, (own_out, other_out), pieces[number][0], logits)
+
+
+def stats_kernel(flows, block, n_chip, wanted, arrived_a, arrived_b, own, other, partial, out, logits):
     core = lax.axis_index("core")
     chip = lax.axis_index("vocab") * n_chip + lax.axis_index("chip")
     width = own.shape[1]
-    blocks = kept.shape[0] // block
-    for part, rows in enumerate((kept, arrived)):
-        for side, columns in enumerate((own, other)):
-            product = jnp.dot(rows[...], columns[...], preferred_element_type=jnp.float32)
-            for number in range(blocks):
-                place = part * blocks + number
-                shift = jnp.where(core == 0, offset(orders[0], place), offset(orders[1], place))
-                first = pl.multiple_of((chip ^ shift) * block, block)
-                logits[pl.ds(first, block), pl.ds(side * width, width)] = product[number * block : (number + 1) * block]
+    logits[...] = partial[...]
+    add_products(flows[0], block, 1, n_chip, arrived_a, (own, other), 0, logits)
+    add_products(flows[1], block, 1, n_chip, arrived_b, (own, other), arrived_a.shape[1], logits)
     values = logits[...]
     highest = jnp.max(values, axis=1, keepdims=True)
     exp_total = jnp.sum(jnp.exp(values - highest), axis=1, keepdims=True)
@@ -87,27 +117,51 @@
     width = unembed.shape[1]
     n_vocab, n_chip = lax.axis_size("vocab"), lax.axis_size("chip")
     n_chips = n_vocab * n_chip
-    orders = gather_orders(n_vocab, n_chip)
+    flows = gather_orders(n_vocab, n_chip)
     core = lax.axis_index("core")
     rows = n_chips * block
 
     other_columns = to_other_core(unembed, n_chips)
-    kept = hidden.reshape(block, depth)
-    for number in range(len(orders[0])):
-        arrived = exchange(kept, (orders[0][number], orders[1][number]), n_chips)
-        if number < len(orders[0]) - 1:
-            kept = jnp.concatenate([kept, arrived], axis=0)
+    cut = depth // 128 * 2 // 3 * 128
+    own_rows = hidden.reshape(block, depth)
+    kept = [own_rows[:, :cut], own_rows[:, cut:]]
+    arrived = [None, None]
+    stages = len(flows[0][0])
+    for number in range(stages):
+        for flow in range(2):
+            masks = (flows[flow][0][number], flows[flow][1][number])
+            arrived[flow] = exchange(kept[flow], masks, n_chips)
+        if number < stages - 1:
+            for flow in range(2):
+                kept[flow] = jnp.concatenate([kept[flow], arrived[flow]], axis=0)
     mine = lax.dynamic_index_in_dim(targets.reshape(heads, n_chips, 2, tok_rows), core, 2, keepdims=False)
     wanted = jnp.transpose(mine, (1, 0, 2)).reshape(rows, 1)
-    held = 2 * (rows + 2 * width) * depth + 4 * rows * (4 * width + 2 * 128 + 8 * n_chips)
+    cost = pl.CostEstimate(
+        flops=2 * rows * width * depth, bytes_accessed=(rows + 4 * width) * depth, transcendentals=0
+    )
+    held = 2 * (rows + 2 * width) * depth + 4 * rows * (8 * width + 2 * 128 + 8 * n_chips)
+    params = pltpu.CompilerParams(vmem_limit_bytes=held + 2**21)
+    in_vmem = pl.BlockSpec(memory_space=pltpu.VMEM)
+    in_place = pl.BlockSpec(memory_space=pl.ANY)
+    columns = jax.ShapeDtypeStruct(unembed.shape, unembed.dtype)
+    own_near, other_near, partial = pl.pallas_call(
+        functools.partial(kept_kernel, flows, block, n_chip),
+        out_shape=(columns, columns, jax.ShapeDtypeStruct((rows, 2 * width), jnp.float32)),
+        in_specs=[in_vmem, in_vmem, in_place, in_place],
+        out_specs=(in_vmem, in_vmem, in_vmem),
+        scratch_shapes=[pltpu.SemaphoreType.DMA((4,))],
+        cost_estimate=cost,
+        compiler_params=params,
+        name="kept",
+    )(kept[0], kept[1], unembed, other_columns)
     sent = pl.pallas_call(
-        functools.partial(stats_kernel, orders, block, n_chip),
+        functools.partial(stats_kernel, flows, block, n_chip),
         out_shape=jax.ShapeDtypeStruct((n_chips, 8, rows), jnp.float32),
         scratch_shapes=[pltpu.VMEM((rows, 2 * width), jnp.float32)],
-        cost_estimate=pl.CostEstimate(flops=4 * rows * width * depth, bytes_accessed=4 * (rows + width) * depth, transcendentals=0),
-        compiler_params=pltpu.CompilerParams(vmem_limit_bytes=held + 2**21),
+        cost_estimate=cost,
+        compiler_params=params,
         name="stats",
-    )(wanted, kept, arrived, unembed, other_columns)
+    )(wanted, arrived[0], arrived[1], own_near, other_near, partial)
     received = lax.all_to_all(sent, CHIPS, split_axis=0, concat_axis=0, tiled=True)
     own_loss, part = pl.pallas_call(
         functools.partial(loss_kernel, n_chip, block, tok_rows),

time: 65.9 us -> 53.3 us (0.81)
  waiting for transfers between devices: 25.3 us -> 10.8 us
  starting transfers between devices: 10.2 us -> 15.8 us
  blocking collectives: 16.1 us -> 12.7 us
  local copies, waits for them, and re-layouts: 5.8 us -> 5.14 us
    ppermute x4 -> x8, waiting for transfers between devices: 25.3 us -> 10.8 us  [exchange(): return lax.ppermute(value, AXES, pairs)]
    ppermute x4 -> x8, starting transfers between devices: 10.2 us -> 15.2 us  [exchange(): return lax.ppermute(value, AXES, pairs)]
    all_to_all x1, blocking collectives: 16.1 us -> 12.7 us  [local(): lax.all_to_all(sent, CHIPS, split_axis=0, concat_axis=0, tiled=True)]
    reshape x1, local copies, waits for them, and re-layouts: 0.79 us -> 0.12 us  [local(): targets.reshape(heads, n_chips, 2, tok_rows)]
    pallas_call x1 -> x2, Pallas kernels: 4.92 us -> 5.18 us  [the longest x1 3.52 us: local(): pl.pallas_call(functools.partial(kept_kernel, flows, block, n_chip), out_...]
    unnamed x5 -> x4, local copies, waits for them, and re-layouts: 2.07 us -> 2.04 us
  transfers between devices with their start and end apart: 6 -> 10, of which waited for: 4 -> 5; matrix products, arithmetic and copies ran while one was open for 4% -> 5% of each run, Pallas kernels for 0% -> 7%
where the time goes in v2:
time: 53.3 us; the launch traced here: 53 us
  starting transfers between devices  15.8 us (30%)
  blocking collectives  12.7 us (24%)
  waiting for transfers between devices  10.8 us (20%)
  Pallas kernels  5.28 us (10%)
  local copies, waits for them, and re-layouts  5.14 us (10%)
  between operations  3.12 us (6%)
    ppermute x8, starting transfers between devices, exchange(): return lax.ppermute(value, AXES, pairs)  15.2 us
    all_to_all x1, blocking collectives, local(): lax.all_to_all(sent, CHIPS, split_axis=0, concat_axis=0, tiled=True)  12.7 us
    ppermute x8, waiting for transfers between devices, exchange(): return lax.ppermute(value, AXES, pairs)  10.8 us
    pallas_call x1, Pallas kernels, local(): pl.pallas_call(functools.partial(kept_kernel, flows, block, n_chip), out_...  3.52 us
    unnamed x4, local copies, waits for them, and re-layouts  2.04 us
    pallas_call x1, Pallas kernels, local(): pl.pallas_call(functools.partial(stats_kernel, flows, block, n_chip), out...  1.65 us
    slice x2, local copies, waits for them, and re-layouts, local(): total = part[0, 0] + to_other_core(part, n_chips)[0, 0]  1.09 us
  transfers between devices with their start and end apart: 10, of which 5 were waited for; matrix products, arithmetic and copies ran while one was open for 5% of the time, Pallas kernels for 7%

profile of v2, /device:TPU:0, one launch (start us, length us, event | category | flops | bytes accessed | tf_op | source)
XLA Modules:
  0.0 53.0 jit_solution(1100410956201320419)
XLA Ops:
  0.6 0.6 %collective-permute-start.8 = (bf16[7168,256]{1,0:T(8,128)(2,1)}, bf16[7168,256]{1,0:T(8,128)(2,1)}, u32[]{:S(2)}, u32[]{:S(2)}) collective-permute-start(bf16[7168,256]{1,0:T(8,128)(2,1)} %own.1), channel_id=1, source_target_pairs={{0,1},{1,0},{2,3},{3,2},{4,5},{5,4},{6,7},{7,6},{8,9},{9,8},{10,11... | collective-permute-start | bytes 11010056 | tf_op jit(solution)/shard_map/ppermute | solution.py:34
  1.2 0.9 %reshape.16 = bf16[8,7168]{1,0:T(8,128)(2,1)S(1)} reshape(bf16[2,4,7168]{2,1,0:T(4,128)(2,1)} %param.3) | data formatting | bytes 229376 | tf_op jit(solution)/shard_map/reshape | solution.py:126
  2.1 3.7 %collective-permute-start = (bf16[8,4736]{1,0:T(8,128)(2,1)S(1)}, bf16[8,4736]{1,0:T(8,128)(2,1)S(1)}, u32[]{:S(2)}, u32[]{:S(2)}) collective-permute-start(bf16[8,4736]{1,0:T(8,128)(2,1)S(1)} %slice.20), channel_id=1, source_target_pairs={{0,16},{1,9},{2,18},{3,11},{4,20},{5,13},{6,22},{7,15},{8,24},{9,1... | collective-permute-start | bytes 227336 | tf_op jit(solution)/shard_map/ppermute | solution.py:29
  5.8 1.5 %collective-permute-start.4 = (bf16[8,2432]{1,0:T(8,128)(2,1)S(1)}, bf16[8,2432]{1,0:T(8,128)(2,1)S(1)}, u32[]{:S(2)}, u32[]{:S(2)}) collective-permute-start(bf16[8,2432]{1,0:T(8,128)(2,1)S(1)} %slice.21), channel_id=1, source_target_pairs={{0,2},{1,5},{2,0},{3,7},{4,6},{5,1},{6,4},{7,3},{8,10},{9,13},{10,... | collective-permute-start | bytes 116744 | tf_op jit(solution)/shard_map/ppermute | solution.py:29
  7.3 0.9 %collective-permute-done = bf16[8,4736]{1,0:T(8,128)(2,1)S(1)} collective-permute-done((bf16[8,4736]{1,0:T(8,128)(2,1)S(1)}, bf16[8,4736]{1,0:T(8,128)(2,1)S(1)}, u32[]{:S(2)}, u32[]{:S(2)}) %collective-permute-start) | collective-permute-done | bytes 75808 | tf_op jit(solution)/shard_map/ppermute | solution.py:29
  8.2 2.4 %collective-permute-start.1 = (bf16[16,4736]{1,0:T(8,128)(2,1)S(1)}, bf16[16,4736]{1,0:T(8,128)(2,1)S(1)}, u32[]{:S(2)}, u32[]{:S(2)}) collective-permute-start(bf16[16,4736]{1,0:T(8,128)(2,1)S(1)} %pad_maximum_fusion.4), channel_id=1, source_target_pairs={{0,8},{1,17},{2,10},{3,19},{4,12},{5,21},{6,14},{7,23},{8,0},{9,25... | collective-permute-start | bytes 454664 | tf_op jit(solution)/shard_map/ppermute | solution.py:29
  10.6 0.0 collective-permute-done.4
  10.6 1.6 %collective-permute-start.5 = (bf16[16,2432]{1,0:T(8,128)(2,1)S(1)}, bf16[16,2432]{1,0:T(8,128)(2,1)S(1)}, u32[]{:S(2)}, u32[]{:S(2)}) collective-permute-start(bf16[16,2432]{1,0:T(8,128)(2,1)S(1)} %pad_maximum_fusion.5), channel_id=1, source_target_pairs={{0,4},{1,3},{2,6},{3,1},{4,0},{5,7},{6,2},{7,5},{8,12},{9,11},{10,... | collective-permute-start | bytes 233480 | tf_op jit(solution)/shard_map/ppermute | solution.py:29
  12.2 2.5 %collective-permute-done.1 = bf16[16,4736]{1,0:T(8,128)(2,1)S(1)} collective-permute-done((bf16[16,4736]{1,0:T(8,128)(2,1)S(1)}, bf16[16,4736]{1,0:T(8,128)(2,1)S(1)}, u32[]{:S(2)}, u32[]{:S(2)}) %collective-permute-start.1) | collective-permute-done | bytes 151584 | tf_op jit(solution)/shard_map/ppermute | solution.py:29
  14.7 0.0 copy-start.1
  14.7 1.8 %collective-permute-start.2 = (bf16[32,4736]{1,0:T(8,128)(2,1)S(1)}, bf16[32,4736]{1,0:T(8,128)(2,1)S(1)}, u32[]{:S(2)}, u32[]{:S(2)}) collective-permute-start(bf16[32,4736]{1,0:T(8,128)(2,1)S(1)} %pad_maximum_fusion.2), channel_id=1, source_target_pairs={{0,2},{1,5},{2,0},{3,7},{4,6},{5,1},{6,4},{7,3},{8,10},{9,13},{10,... | collective-permute-start | bytes 909320 | tf_op jit(solution)/shard_map/ppermute | solution.py:29
  16.5 0.0 collective-permute-done.5
  16.5 2.0 %collective-permute-start.6 = (bf16[32,2432]{1,0:T(8,128)(2,1)S(1)}, bf16[32,2432]{1,0:T(8,128)(2,1)S(1)}, u32[]{:S(2)}, u32[]{:S(2)}) collective-permute-start(bf16[32,2432]{1,0:T(8,128)(2,1)S(1)} %pad_maximum_fusion.3), channel_id=1, source_target_pairs={{0,16},{1,9},{2,18},{3,11},{4,20},{5,13},{6,22},{7,15},{8,24},{9,1... | collective-permute-start | bytes 466952 | tf_op jit(solution)/shard_map/ppermute | solution.py:29
  18.5 3.1 %collective-permute-done.2 = bf16[32,4736]{1,0:T(8,128)(2,1)S(1)} collective-permute-done((bf16[32,4736]{1,0:T(8,128)(2,1)S(1)}, bf16[32,4736]{1,0:T(8,128)(2,1)S(1)}, u32[]{:S(2)}, u32[]{:S(2)}) %collective-permute-start.2) | collective-permute-done | bytes 303136 | tf_op jit(solution)/shard_map/ppermute | solution.py:29
  21.6 0.1 pad_maximum_fusion.kept_a
  21.7 1.8 %collective-permute-start.3 = (bf16[64,4736]{1,0:T(8,128)(2,1)S(1)}, bf16[64,4736]{1,0:T(8,128)(2,1)S(1)}, u32[]{:S(2)}, u32[]{:S(2)}) collective-permute-start(bf16[64,4736]{1,0:T(8,128)(2,1)S(1)} %pad_maximum_fusion.kept_a), channel_id=1, source_target_pairs={{0,4},{1,3},{2,6},{3,1},{4,0},{5,7},{6,2},{7,5},{8,12},{9,11},{10,... | collective-permute-start | bytes 1818632 | tf_op jit(solution)/shard_map/ppermute | solution.py:29
  23.5 0.9 %collective-permute-done.6 = bf16[32,2432]{1,0:T(8,128)(2,1)S(1)} collective-permute-done((bf16[32,2432]{1,0:T(8,128)(2,1)S(1)}, bf16[32,2432]{1,0:T(8,128)(2,1)S(1)}, u32[]{:S(2)}, u32[]{:S(2)}) %collective-permute-start.6) | collective-permute-done | bytes 155680 | tf_op jit(solution)/shard_map/ppermute | solution.py:29
  24.4 0.4 collective-permute-start.7
  24.9 0.0 copy-done.1
  24.9 0.1 reshape.14
  25.0 0.1 copy.8
  25.1 0.1 copy.9
  25.2 0.1 reshape.17.wanted
  25.3 0.0 collective-permute-done.8.other
  25.3 0.0 copy-start
  25.3 2.0 %copy-done = bf16[7168,256]{1,0:T(8,128)(2,1)S(1)} copy-done((bf16[7168,256]{1,0:T(8,128)(2,1)S(1)}, bf16[7168,256]{1,0:T(8,128)(2,1)}, u32[]{:S(2)}) %copy-start) | copy-done | bytes 3670040
  27.4 3.5 %kept.1 = (bf16[7168,256]{1,0:T(8,128)(2,1)S(1)}, bf16[7168,256]{1,0:T(8,128)(2,1)S(1)}, f32[128,512]{1,0:T(8,128)S(1)}) custom-call(bf16[64,4736]{1,0:T(8,128)(2,1)S(1)} %pad_maximum_fusion.kept_a, bf16[64,2432]{1,0:T(8,128)(2,1)S(1)} %pad_maximum_fusion.1.kept_b, bf16[7168,256]{1,0:T(8,128)(2,1)S(1)} %copy-done, bf16[7168,256]{1,0:T(8,128)(2,1)} %collective-permute-done.8.other), custom_call_target="tpu_custom_call" | custom-call | flops 469762048 | bytes 8257536 | tf_op jit(solution)/shard_map/kept/pallas_call | solution.py:147
  30.9 3.5 %collective-permute-done.7.arrived_b = bf16[64,2432]{1,0:T(8,128)(2,1)S(1)} collective-permute-done((bf16[64,2432]{1,0:T(8,128)(2,1)S(1)}, bf16[64,2432]{1,0:T(8,128)(2,1)S(1)}, u32[]{:S(2)}, u32[]{:S(2)}) %collective-permute-start.7) | collective-permute-done | bytes 311328 | tf_op jit(solution)/shard_map/ppermute | solution.py:29
  34.3 0.0 collective-permute-done.3.arrived_a
  34.3 1.7 %stats.1 = f32[16,8,128]{2,1,0:T(8,128)S(1)} custom-call(s32[128,1]{1,0:T(8,128)S(1)} %reshape.17.wanted, bf16[64,4736]{1,0:T(8,128)(2,1)S(1)} %collective-permute-done.3.arrived_a, bf16[64,2432]{1,0:T(8,128)(2,1)S(1)} %collective-permute-done.7.arrived_b, bf16[7168,256]{1,0:T(8,128)(2,1)S(1)} %get-tuple-element.7.own, ...), custom_call_target="tpu_custom_call" | custom-call | flops 469762048 | bytes 8257536 | tf_op jit(solution)/shard_map/stats/pallas_call | solution.py:157
  36.0 12.7 %all_to_all.5.received = f32[16,8,128]{2,1,0:T(8,128)S(1)} all-to-all(f32[16,8,128]{2,1,0:T(8,128)S(1)} %stats.1), channel_id=1, replica_groups=mesh['vocab'=8,'chip'=2,'core'=2] {'vocab','chip'}, dimensions={0} | all-to-all | bytes 131072 | tf_op jit(solution)/shard_map/all_to_all | solution.py:165
  48.7 0.1 loss.1
  48.8 0.0 collective-permute-start.9
  48.9 0.5 slice.18
  49.4 0.6 %reshape_squeeze.3 = f32[2,4]{1,0:T(2,128)} reshape(f32[8]{0:T(128)S(1)} %slice_reduce_fusion) | data formatting | bytes 64 | tf_op jit(solution)/shard_map/reshape;squeeze | solution.py:172
  50.0 0.0 collective-permute-done.9
  50.0 0.6 %slice.19 = f32[1,1]{1,0:T(1,128)} slice(f32[8,128]{1,0:T(8,128)S(1)} %collective-permute-done.9), slice={[0:1], [0:1]} | slice | bytes 8 | tf_op jit(solution)/shard_map/slice | solution.py:173
  (9 shorter events, 0.1 us)
Async XLA Ops:
  0.6 24.7 %collective-permute-start.8 = (bf16[7168,256]{1,0:T(8,128)(2,1)}, bf16[7168,256]{1,0:T(8,128)(2,1)}, u32[]{:S(2)}, u32[]{:S(2)}) collective-permute-start(bf16[7168,256]{1,0:T(8,128)(2,1)} %own.1), channel_id=1, source_target_pairs={{0,1},{1,0},{2,3},{3,2},{4,5},{5,4},{6,7},{7,6},{8,9},{9,8},{10,11... | collective-permute-start | bytes 11010056 | tf_op jit(solution)/shard_map/ppermute | solution.py:34
  2.1 6.0 %collective-permute-start = (bf16[8,4736]{1,0:T(8,128)(2,1)S(1)}, bf16[8,4736]{1,0:T(8,128)(2,1)S(1)}, u32[]{:S(2)}, u32[]{:S(2)}) collective-permute-start(bf16[8,4736]{1,0:T(8,128)(2,1)S(1)} %slice.20), channel_id=1, source_target_pairs={{0,16},{1,9},{2,18},{3,11},{4,20},{5,13},{6,22},{7,15},{8,24},{9,1... | collective-permute-start | bytes 227336 | tf_op jit(solution)/shard_map/ppermute | solution.py:29
  5.8 4.8 %collective-permute-start.4 = (bf16[8,2432]{1,0:T(8,128)(2,1)S(1)}, bf16[8,2432]{1,0:T(8,128)(2,1)S(1)}, u32[]{:S(2)}, u32[]{:S(2)}) collective-permute-start(bf16[8,2432]{1,0:T(8,128)(2,1)S(1)} %slice.21), channel_id=1, source_target_pairs={{0,2},{1,5},{2,0},{3,7},{4,6},{5,1},{6,4},{7,3},{8,10},{9,13},{10,... | collective-permute-start | bytes 116744 | tf_op jit(solution)/shard_map/ppermute | solution.py:29
  8.2 6.5 %collective-permute-start.1 = (bf16[16,4736]{1,0:T(8,128)(2,1)S(1)}, bf16[16,4736]{1,0:T(8,128)(2,1)S(1)}, u32[]{:S(2)}, u32[]{:S(2)}) collective-permute-start(bf16[16,4736]{1,0:T(8,128)(2,1)S(1)} %pad_maximum_fusion.4), channel_id=1, source_target_pairs={{0,8},{1,17},{2,10},{3,19},{4,12},{5,21},{6,14},{7,23},{8,0},{9,25... | collective-permute-start | bytes 454664 | tf_op jit(solution)/shard_map/ppermute | solution.py:29
  10.6 5.9 %collective-permute-start.5 = (bf16[16,2432]{1,0:T(8,128)(2,1)S(1)}, bf16[16,2432]{1,0:T(8,128)(2,1)S(1)}, u32[]{:S(2)}, u32[]{:S(2)}) collective-permute-start(bf16[16,2432]{1,0:T(8,128)(2,1)S(1)} %pad_maximum_fusion.5), channel_id=1, source_target_pairs={{0,4},{1,3},{2,6},{3,1},{4,0},{5,7},{6,2},{7,5},{8,12},{9,11},{10,... | collective-permute-start | bytes 233480 | tf_op jit(solution)/shard_map/ppermute | solution.py:29
  14.7 10.2 %copy-start.1 = (s32[2,128]{1,0:T(2,128)S(1)}, s32[2,128]{1,0:T(2,128)}, u32[]{:S(2)}) copy-start(s32[2,128]{1,0:T(2,128)} %param.5) | copy-start | bytes 3076
  14.7 6.9 %collective-permute-start.2 = (bf16[32,4736]{1,0:T(8,128)(2,1)S(1)}, bf16[32,4736]{1,0:T(8,128)(2,1)S(1)}, u32[]{:S(2)}, u32[]{:S(2)}) collective-permute-start(bf16[32,4736]{1,0:T(8,128)(2,1)S(1)} %pad_maximum_fusion.2), channel_id=1, source_target_pairs={{0,2},{1,5},{2,0},{3,7},{4,6},{5,1},{6,4},{7,3},{8,10},{9,13},{10,... | collective-permute-start | bytes 909320 | tf_op jit(solution)/shard_map/ppermute | solution.py:29
  16.5 7.9 %collective-permute-start.6 = (bf16[32,2432]{1,0:T(8,128)(2,1)S(1)}, bf16[32,2432]{1,0:T(8,128)(2,1)S(1)}, u32[]{:S(2)}, u32[]{:S(2)}) collective-permute-start(bf16[32,2432]{1,0:T(8,128)(2,1)S(1)} %pad_maximum_fusion.3), channel_id=1, source_target_pairs={{0,16},{1,9},{2,18},{3,11},{4,20},{5,13},{6,22},{7,15},{8,24},{9,1... | collective-permute-start | bytes 466952 | tf_op jit(solution)/shard_map/ppermute | solution.py:29
  21.7 12.7 %collective-permute-start.3 = (bf16[64,4736]{1,0:T(8,128)(2,1)S(1)}, bf16[64,4736]{1,0:T(8,128)(2,1)S(1)}, u32[]{:S(2)}, u32[]{:S(2)}) collective-permute-start(bf16[64,4736]{1,0:T(8,128)(2,1)S(1)} %pad_maximum_fusion.kept_a), channel_id=1, source_target_pairs={{0,4},{1,3},{2,6},{3,1},{4,0},{5,7},{6,2},{7,5},{8,12},{9,11},{10,... | collective-permute-start | bytes 1818632 | tf_op jit(solution)/shard_map/ppermute | solution.py:29
  24.4 9.9 %collective-permute-start.7 = (bf16[64,2432]{1,0:T(8,128)(2,1)S(1)}, bf16[64,2432]{1,0:T(8,128)(2,1)S(1)}, u32[]{:S(2)}, u32[]{:S(2)}) collective-permute-start(bf16[64,2432]{1,0:T(8,128)(2,1)S(1)} %pad_maximum_fusion.1.kept_b), channel_id=1, source_target_pairs={{0,8},{1,17},{2,10},{3,19},{4,12},{5,21},{6,14},{7,23},{8,0},{9,25... | collective-permute-start | bytes 933896 | tf_op jit(solution)/shard_map/ppermute | solution.py:29
  25.3 2.0 %copy-start = (bf16[7168,256]{1,0:T(8,128)(2,1)S(1)}, bf16[7168,256]{1,0:T(8,128)(2,1)}, u32[]{:S(2)}) copy-start(bf16[7168,256]{1,0:T(8,128)(2,1)} %own.1) | copy-start | bytes 11010052
  48.8 1.2 %collective-permute-start.9 = (f32[8,128]{1,0:T(8,128)S(1)}, f32[8,128]{1,0:T(8,128)S(1)}, u32[]{:S(2)}, u32[]{:S(2)}) collective-permute-start(f32[8,128]{1,0:T(8,128)S(1)} %get-tuple-element.11), channel_id=1, source_target_pairs={{0,1},{1,0},{2,3},{3,2},{4,5},{5,4},{6,7},{7,6},{8,9},{9,8},{10,11... | collective-permute-start | bytes 12296 | tf_op jit(solution)/shard_map/ppermute | solution.py:34

commit v3 on v2

v3 whole, which is shorter than its diff:
```python
import functools
import jax
import jax.numpy as jnp
from jax import lax
from jax.experimental import pallas as pl
from jax.experimental.pallas import tpu as pltpu
from jax.sharding import Mesh, PartitionSpec as P

MTP_WEIGHT = 0.3
AXES = ("vocab", "chip", "core")
CHIPS = ("vocab", "chip")


def bits(count):
    return [1 << place for place in range(count.bit_length() - 1)]


def gather_orders(n_vocab, n_chip):
    near = bits(n_chip) + [n_chip * mask for mask in bits(n_vocab)[:1]]
    far = [n_chip * mask for mask in bits(n_vocab)[1:]]
    return (
        (far[::-1] + near, far + near[::-1]),
        (near + far[::-1], near[::-1] + far),
    )


def exchange(value, masks, n_chips):
    pairs = [(2 * chip + core, 2 * (chip ^ masks[core]) + core) for chip in range(n_chips) for core in range(2)]
    return lax.ppermute(value, AXES, pairs)


def to_other_core(value, n_chips):
    pairs = [(source, source ^ 1) for source in range(2 * n_chips)]
    return lax.ppermute(value, AXES, pairs)


def offset(masks, place):
    total = 0
    for number, mask in enumerate(masks):
        if place >> number & 1:
            total ^= mask
    return total


def add_products(orders, block, part, n_chip, rows, columns, side, first_depth, logits):
    core = lax.axis_index("core")
    chip = lax.axis_index("vocab") * n_chip + lax.axis_index("chip")
    blocks, width = rows.shape[0] // block, columns.shape[1]
    product = jnp.dot(
        rows[...], columns[pl.ds(first_depth, rows.shape[1]), :], preferred_element_type=jnp.float32
    )
    for number in range(blocks):
        place = part * blocks + number
        shift = jnp.where(core == 0, offset(orders[0], place), offset(orders[1], place))
        first = pl.multiple_of((chip ^ shift) * block, block)
        target = (pl.ds(first, block), pl.ds(side * width, width))
        logits[target] = logits[target] + product[number * block : (number + 1) * block]


def kept_kernel(flows, block, n_chip, kept_a, kept_b, own, other, other_out, logits, arrivals):
    cut, depth = kept_a.shape[1], own.shape[0]
    flow_rows = ((kept_a, 0), (kept_b, cut))
    copies = []
    for number, (first, count) in enumerate(((0, cut), (cut, depth - cut))):
        span = pl.ds(first, count)
        copies.append(pltpu.make_async_copy(other.at[span], other_out.at[span], arrivals.at[number]))
    for copy in copies:
        copy.start()
    logits[...] = jnp.zeros_like(logits)
    for number, (kept, first) in enumerate(flow_rows):
        add_products(flows[number], block, 0, n_chip, kept, own, 0, first, logits)
    for number, (kept, first) in enumerate(flow_rows):
        copies[number].wait()
        add_products(flows[number], block, 0, n_chip, kept, other_out, 1, first, logits)


def first_kernel(flows, block, n_chip, arrived, own, other, partial, logits):
    logits[...] = partial[...]
    for side, columns in enumerate((own, other)):
        add_products(flows[0], block, 1, n_chip, arrived, columns, side, 0, logits)


def stats_kernel(flows, block, n_chip, wanted, arrived, own, other, partial, out, logits):
    core = lax.axis_index("core")
    chip = lax.axis_index("vocab") * n_chip + lax.axis_index("chip")
    width = own.shape[1]
    logits[...] = partial[...]
    for side, columns in enumerate((own, other)):
        add_products(flows[1], block, 1, n_chip, arrived, columns, side, own.shape[0] - arrived.shape[1], logits)
    values = logits[...]
    highest = jnp.max(values, axis=1, keepdims=True)
    exp_total = jnp.sum(jnp.exp(values - highest), axis=1, keepdims=True)
    device = 2 * chip + core
    lane = lax.broadcasted_iota(jnp.int32, values.shape, 1)
    column_ids = jnp.where(lane < width, device * width + lane, (device ^ 1) * width + lane - width)
    picked = jnp.sum(jnp.where(column_ids == wanted[...], values, 0.0), axis=1, keepdims=True)
    member = lax.broadcasted_iota(jnp.int32, (values.shape[0], 128), 1)
    table = jnp.where(member == 0, highest + jnp.log(exp_total), picked)
    sent = jnp.transpose(table)[:2]
    for chip_number in range(out.shape[0]):
        out[chip_number] = sent


def loss_kernel(n_chip, block, tok_rows, received, own_loss, part):
    chip = lax.axis_index("vocab") * n_chip + lax.axis_index("chip")
    rows = received.shape[2]
    log_sums = received[:, 0, :]
    highest = jnp.max(log_sums, axis=0, keepdims=True)
    exp_total = jnp.sum(jnp.exp(log_sums - highest), axis=0, keepdims=True)
    picked = jnp.sum(received[:, 1, :], axis=0, keepdims=True)
    loss = highest + jnp.log(exp_total) - picked
    lane = lax.broadcasted_iota(jnp.int32, loss.shape, 1)
    weight = jnp.where(lane // tok_rows % 2 == 0, 1.0 / rows, MTP_WEIGHT / rows)
    part[...] = jnp.sum(loss * weight, axis=1, keepdims=True)
    repeated = jnp.broadcast_to(loss, (8, rows))
    for head in range(2):
        turned = pltpu.roll(repeated, rows - chip * block - head * tok_rows, 1)
        own_loss[pl.ds(head, 1), :] = turned[:1, :tok_rows]


def local(hidden, unembed, targets):
    heads, tok_rows, depth = hidden.shape
    block = heads * tok_rows
    width = unembed.shape[1]
    n_vocab, n_chip = lax.axis_size("vocab"), lax.axis_size("chip")
    n_chips = n_vocab * n_chip
    flows = gather_orders(n_vocab, n_chip)
    core = lax.axis_index("core")
    rows = n_chips * block

    cut = depth // 128 * 2 // 3 * 128
    own_rows = hidden.reshape(block, depth)
    kept = [own_rows[:, :cut], own_rows[:, cut:]]
    arrived = [None, None]
    stages = len(flows[0][0])
    for number in range(stages):
        for flow in range(2):
            masks = (flows[flow][0][number], flows[flow][1][number])
            arrived[flow] = exchange(kept[flow], masks, n_chips)
        if number == 0:
            later_columns, _ = lax.optimization_barrier((unembed, arrived))
            other_columns = to_other_core(later_columns, n_chips)
        if number < stages - 1:
            for flow in range(2):
                kept[flow] = jnp.concatenate([kept[flow], arrived[flow]], axis=0)
    mine = lax.dynamic_index_in_dim(targets.reshape(heads, n_chips, 2, tok_rows), core, 2, keepdims=False)
    wanted = jnp.transpose(mine, (1, 0, 2)).reshape(rows, 1)
    cost = pl.CostEstimate(
        flops=2 * rows * width * depth, bytes_accessed=(rows + 4 * width) * depth, transcendentals=0
    )
    held = 2 * (rows + 2 * width) * depth + 4 * rows * (8 * width + 2 * 128 + 8 * n_chips)
    params = pltpu.CompilerParams(vmem_limit_bytes=held + 2**21)
    in_vmem = pl.BlockSpec(memory_space=pltpu.VMEM)
    in_hbm = pl.BlockSpec(memory_space=pltpu.HBM)
    columns = jax.ShapeDtypeStruct(unembed.shape, unembed.dtype)
    other_near, partial = pl.pallas_call(
        functools.partial(kept_kernel, flows, block, n_chip),
        out_shape=(columns, jax.ShapeDtypeStruct((rows, 2 * width), jnp.float32)),
        in_specs=[in_vmem, in_vmem, in_vmem, in_hbm],
        out_specs=(in_vmem, in_vmem),
        scratch_shapes=[pltpu.SemaphoreType.DMA((2,))],
        cost_estimate=cost,
        compiler_params=params,
        name="kept",
    )(kept[0], kept[1], unembed, other_columns)
    logits = jax.ShapeDtypeStruct((rows, 2 * width), jnp.float32)
    partial = pl.pallas_call(
        functools.partial(first_kernel, flows, block, n_chip),
        out_shape=logits,
        cost_estimate=cost,
        compiler_params=params,
        name="first",
    )(arrived[0], unembed, other_near, partial)
    sent = pl.pallas_call(
        functools.partial(stats_kernel, flows, block, n_chip),
        out_shape=jax.ShapeDtypeStruct((n_chips, 2, rows), jnp.float32),
        scratch_shapes=[pltpu.VMEM((rows, 2 * width), jnp.float32)],
        cost_estimate=cost,
        compiler_params=params,
        name="stats",
    )(wanted, arrived[1], unembed, other_near, partial)
    received = lax.all_to_all(sent, CHIPS, split_axis=0, concat_axis=0, tiled=True)
    token_loss, part = pl.pallas_call(
        functools.partial(loss_kernel, n_chip, block, tok_rows),
        out_shape=(jax.ShapeDtypeStruct((heads, tok_rows), jnp.float32), jax.ShapeDtypeStruct((1, 1), jnp.float32)),
        compiler_params=pltpu.CompilerParams(vmem_limit_bytes=2**20 + 4 * 4 * n_chips * 8 * rows),
        name="loss",
    )(received)
    total = (part + to_other_core(part, n_chips)).reshape(())
    return token_loss, total


def solution(mesh):
    n_vocab, n_data = mesh.shape["vocab"], mesh.shape["dp"]
    fine = Mesh(mesh.devices.reshape(n_vocab, n_data // 2, 2), AXES)
    return jax.shard_map(
        local,
        mesh=fine,
        in_specs=(P(None, AXES, None), P(None, AXES), P()),
        out_specs=(P(None, AXES), P()),
        check_vma=False,
    )
```

time: 53.3 us -> 53.5 us (level)
  waiting for transfers between devices: 10.8 us -> 13.6 us
  starting transfers between devices: 15.8 us -> 13.1 us
  local copies, waits for them, and re-layouts: 5.14 us -> 3.4 us
  Pallas kernels: 5.28 us -> 6.54 us
  blocking collectives: 12.7 us -> 13.3 us
    ppermute x8, starting transfers between devices: 15.2 us -> 13.1 us  [exchange(): return lax.ppermute(value, AXES, pairs)]
    ppermute x8, waiting for transfers between devices: 10.8 us -> 12.4 us  [exchange(): return lax.ppermute(value, AXES, pairs)]
    ppermute x2, waiting for transfers between devices: 0.01 us -> 1.27 us  [to_other_core(): return lax.ppermute(value, AXES, pairs)]
    slice x3 -> x0, local copies, waits for them, and re-layouts: 1.11 us -> none  [the longest x2 1.09 us: local(): total = part[0, 0] + to_other_core(part, n_chips)[0, 0]]
    pallas_call x0 -> x1, Pallas kernels: none -> 0.98 us  [local(): pl.pallas_call(functools.partial(first_kernel, flows, block, n_chip), out...]
    pallas_call x1, Pallas kernels: 1.65 us -> 0.82 us  [local(): pl.pallas_call(functools.partial(stats_kernel, flows, block, n_chip), out...]
    another operation x1 -> x0, local copies, waits for them, and re-layouts: 0.64 us -> none  [local(): token_loss = own_loss[0, :block].reshape(heads, tok_rows)]
    pallas_call x1, Pallas kernels: 0.1 us -> 0.68 us  [local(): pl.pallas_call(functools.partial(loss_kernel, n_chip, block, tok_rows), o...]
  transfers between devices with their start and end apart: 10 -> 10, of which waited for: 5 -> 7; matrix products, arithmetic and copies ran while one was open for 5% -> 1% of each run, Pallas kernels for 7% -> 9%
where the time goes in v3:
time: 53.5 us; the launch traced here: 53.3 us
  waiting for transfers between devices  13.6 us (25%)
  blocking collectives  13.3 us (25%)
  starting transfers between devices  13.1 us (24%)
  Pallas kernels  6.54 us (12%)
  local copies, waits for them, and re-layouts  3.4 us (6%)
  between operations  3.15 us (6%)
    all_to_all x1, blocking collectives, local(): lax.all_to_all(sent, CHIPS, split_axis=0, concat_axis=0, tiled=True)  13.3 us
    ppermute x8, starting transfers between devices, exchange(): return lax.ppermute(value, AXES, pairs)  13.1 us
    ppermute x8, waiting for transfers between devices, exchange(): return lax.ppermute(value, AXES, pairs)  12.4 us
    pallas_call x1, Pallas kernels, local(): pl.pallas_call(functools.partial(kept_kernel, flows, block, n_chip), out_...  4.06 us
    unnamed x6, local copies, waits for them, and re-layouts  2.04 us
    ppermute x2, waiting for transfers between devices, to_other_core(): return lax.ppermute(value, AXES, pairs)  1.27 us
  transfers between devices with their start and end apart: 10, of which 7 were waited for; matrix products, arithmetic and copies ran while one was open for 1% of the time, Pallas kernels for 9%

profile of v3, /device:TPU:0, one launch (start us, length us, event | category | flops | bytes accessed | tf_op | source)
XLA Modules:
  0.0 53.3 jit_solution(17660116382005998117)
XLA Ops:
  0.6 0.9 %reshape.18 = bf16[8,7168]{1,0:T(8,128)(2,1)S(1)} reshape(bf16[2,4,7168]{2,1,0:T(4,128)(2,1)} %param.3) | data formatting | bytes 229376 | tf_op jit(solution)/shard_map/reshape | solution.py:132
  1.6 4.1 %collective-permute-start.4 = (bf16[8,4736]{1,0:T(8,128)(2,1)S(1)}, bf16[8,4736]{1,0:T(8,128)(2,1)S(1)}, u32[]{:S(2)}, u32[]{:S(2)}) collective-permute-start(bf16[8,4736]{1,0:T(8,128)(2,1)S(1)} %slice.9), channel_id=1, source_target_pairs={{0,16},{1,9},{2,18},{3,11},{4,20},{5,13},{6,22},{7,15},{8,24},{9,1... | collective-permute-start | bytes 227336 | tf_op jit(solution)/shard_map/ppermute | solution.py:29
  5.7 1.5 %collective-permute-start = (bf16[8,2432]{1,0:T(8,128)(2,1)S(1)}, bf16[8,2432]{1,0:T(8,128)(2,1)S(1)}, u32[]{:S(2)}, u32[]{:S(2)}) collective-permute-start(bf16[8,2432]{1,0:T(8,128)(2,1)S(1)} %slice.8), channel_id=1, source_target_pairs={{0,2},{1,5},{2,0},{3,7},{4,6},{5,1},{6,4},{7,3},{8,10},{9,13},{10,... | collective-permute-start | bytes 116744 | tf_op jit(solution)/shard_map/ppermute | solution.py:29
  7.2 2.5 %collective-permute-done = bf16[8,2432]{1,0:T(8,128)(2,1)S(1)} collective-permute-done((bf16[8,2432]{1,0:T(8,128)(2,1)S(1)}, bf16[8,2432]{1,0:T(8,128)(2,1)S(1)}, u32[]{:S(2)}, u32[]{:S(2)}) %collective-permute-start) | collective-permute-done | bytes 38944 | tf_op jit(solution)/shard_map/ppermute | solution.py:29
  9.7 0.0 collective-permute-done.4
  9.7 0.0 collective-permute-start.7
  9.7 1.6 %collective-permute-start.5 = (bf16[16,4736]{1,0:T(8,128)(2,1)S(1)}, bf16[16,4736]{1,0:T(8,128)(2,1)S(1)}, u32[]{:S(2)}, u32[]{:S(2)}) collective-permute-start(bf16[16,4736]{1,0:T(8,128)(2,1)S(1)} %pad_maximum_fusion.4), channel_id=1, source_target_pairs={{0,8},{1,17},{2,10},{3,19},{4,12},{5,21},{6,14},{7,23},{8,0},{9,25... | collective-permute-start | bytes 454664 | tf_op jit(solution)/shard_map/ppermute | solution.py:29
  11.4 1.5 %collective-permute-start.1 = (bf16[16,2432]{1,0:T(8,128)(2,1)S(1)}, bf16[16,2432]{1,0:T(8,128)(2,1)S(1)}, u32[]{:S(2)}, u32[]{:S(2)}) collective-permute-start(bf16[16,2432]{1,0:T(8,128)(2,1)S(1)} %pad_maximum_fusion.5), channel_id=1, source_target_pairs={{0,4},{1,3},{2,6},{3,1},{4,0},{5,7},{6,2},{7,5},{8,12},{9,11},{10,... | collective-permute-start | bytes 233480 | tf_op jit(solution)/shard_map/ppermute | solution.py:29
  12.9 3.7 %collective-permute-done.5 = bf16[16,4736]{1,0:T(8,128)(2,1)S(1)} collective-permute-done((bf16[16,4736]{1,0:T(8,128)(2,1)S(1)}, bf16[16,4736]{1,0:T(8,128)(2,1)S(1)}, u32[]{:S(2)}, u32[]{:S(2)}) %collective-permute-start.5) | collective-permute-done | bytes 151584 | tf_op jit(solution)/shard_map/ppermute | solution.py:29
  16.6 0.0 copy-start.2
  16.6 1.6 %collective-permute-start.6 = (bf16[32,4736]{1,0:T(8,128)(2,1)S(1)}, bf16[32,4736]{1,0:T(8,128)(2,1)S(1)}, u32[]{:S(2)}, u32[]{:S(2)}) collective-permute-start(bf16[32,4736]{1,0:T(8,128)(2,1)S(1)} %pad_maximum_fusion.2), channel_id=1, source_target_pairs={{0,2},{1,5},{2,0},{3,7},{4,6},{5,1},{6,4},{7,3},{8,10},{9,13},{10,... | collective-permute-start | bytes 909320 | tf_op jit(solution)/shard_map/ppermute | solution.py:29
  18.2 0.0 collective-permute-done.1
  18.2 1.1 %collective-permute-start.2 = (bf16[32,2432]{1,0:T(8,128)(2,1)S(1)}, bf16[32,2432]{1,0:T(8,128)(2,1)S(1)}, u32[]{:S(2)}, u32[]{:S(2)}) collective-permute-start(bf16[32,2432]{1,0:T(8,128)(2,1)S(1)} %pad_maximum_fusion.3), channel_id=1, source_target_pairs={{0,16},{1,9},{2,18},{3,11},{4,20},{5,13},{6,22},{7,15},{8,24},{9,1... | collective-permute-start | bytes 466952 | tf_op jit(solution)/shard_map/ppermute | solution.py:29
  19.3 4.2 %collective-permute-done.6 = bf16[32,4736]{1,0:T(8,128)(2,1)S(1)} collective-permute-done((bf16[32,4736]{1,0:T(8,128)(2,1)S(1)}, bf16[32,4736]{1,0:T(8,128)(2,1)S(1)}, u32[]{:S(2)}, u32[]{:S(2)}) %collective-permute-start.6) | collective-permute-done | bytes 303136 | tf_op jit(solution)/shard_map/ppermute | solution.py:29
  23.5 0.1 pad_maximum_fusion.kept_a
  23.6 1.6 %collective-permute-start.8 = (bf16[64,4736]{1,0:T(8,128)(2,1)S(1)}, bf16[64,4736]{1,0:T(8,128)(2,1)S(1)}, u32[]{:S(2)}, u32[]{:S(2)}) collective-permute-start(bf16[64,4736]{1,0:T(8,128)(2,1)S(1)} %pad_maximum_fusion.kept_a), channel_id=1, source_target_pairs={{0,4},{1,3},{2,6},{3,1},{4,0},{5,7},{6,2},{7,5},{8,12},{9,11},{10,... | collective-permute-start | bytes 1818632 | tf_op jit(solution)/shard_map/ppermute | solution.py:29
  25.2 0.9 %collective-permute-done.2 = bf16[32,2432]{1,0:T(8,128)(2,1)S(1)} collective-permute-done((bf16[32,2432]{1,0:T(8,128)(2,1)S(1)}, bf16[32,2432]{1,0:T(8,128)(2,1)S(1)}, u32[]{:S(2)}, u32[]{:S(2)}) %collective-permute-start.2) | collective-permute-done | bytes 155680 | tf_op jit(solution)/shard_map/ppermute | solution.py:29
  26.1 0.1 collective-permute-start.3
  26.2 0.0 copy-done.2
  26.2 0.1 reshape.16
  26.3 0.1 copy.8
  26.4 0.1 copy.9
  26.5 0.1 reshape.20.wanted
  26.6 0.0 collective-permute-done.7.other
  26.6 0.0 copy-start
  26.7 2.0 %copy-done = bf16[7168,256]{1,0:T(8,128)(2,1)S(1)} copy-done((bf16[7168,256]{1,0:T(8,128)(2,1)S(1)}, bf16[7168,256]{1,0:T(8,128)(2,1)}, u32[]{:S(2)}) %copy-start) | copy-done | bytes 3670040
  28.7 0.0 copy-start.1
  28.7 4.1 %kept.1 = (bf16[7168,256]{1,0:T(8,128)(2,1)S(1)}, f32[128,512]{1,0:T(8,128)S(1)}) custom-call(bf16[64,4736]{1,0:T(8,128)(2,1)S(1)} %pad_maximum_fusion.kept_a, bf16[64,2432]{1,0:T(8,128)(2,1)S(1)} %pad_maximum_fusion.1.kept_b, bf16[7168,256]{1,0:T(8,128)(2,1)S(1)} %copy-done, bf16[7168,256]{1,0:T(8,128)(2,1)} %collective-permute-done.7.other), custom_call_target="tpu_custom_call" | custom-call | flops 469762048 | bytes 8257536 | tf_op jit(solution)/shard_map/kept/pallas_call | solution.py:156
  32.8 0.9 %collective-permute-done.8.arrived = bf16[64,4736]{1,0:T(8,128)(2,1)S(1)} collective-permute-done((bf16[64,4736]{1,0:T(8,128)(2,1)S(1)}, bf16[64,4736]{1,0:T(8,128)(2,1)S(1)}, u32[]{:S(2)}, u32[]{:S(2)}) %collective-permute-start.8) | collective-permute-done | bytes 606240 | tf_op jit(solution)/shard_map/ppermute | solution.py:29
  33.7 0.0 copy-done.1
  33.7 1.0 %first.1.partial = f32[128,512]{1,0:T(8,128)S(1)} custom-call(bf16[64,4736]{1,0:T(8,128)(2,1)S(1)} %collective-permute-done.8.arrived, bf16[7168,256]{1,0:T(8,128)(2,1)S(1)} %copy-done.1, bf16[7168,256]{1,0:T(8,128)(2,1)S(1)} %get-tuple-element.8.other, f32[128,512]{1,0:T(8,128)S(1)} %get-tuple-element.9.partial), custom_call_target="tpu_custom_call" | custom-call | flops 469762048 | bytes 8257536 | tf_op jit(solution)/shard_map/first/pallas_call | solution.py:167
  34.7 0.1 collective-permute-done.3.arrived
  34.8 0.8 %stats.1 = f32[16,2,128]{2,1,0:T(2,128)S(1)} custom-call(s32[128,1]{1,0:T(8,128)S(1)} %reshape.20.wanted, bf16[64,2432]{1,0:T(8,128)(2,1)S(1)} %collective-permute-done.3.arrived, bf16[7168,256]{1,0:T(8,128)(2,1)S(1)} %copy-done.1, bf16[7168,256]{1,0:T(8,128)(2,1)S(1)} %get-tuple-element.8.other, f32[128,512]{1,0:T(8,128)S(1)} %first.1.partial), custom_call_target="tpu_custom_call" | custom-call | flops 469762048 | bytes 8257536 | tf_op jit(solution)/shard_map/stats/pallas_call | solution.py:174
  35.7 13.3 %all_to_all.5.received = f32[16,2,128]{2,1,0:T(2,128)S(1)} all-to-all(f32[16,2,128]{2,1,0:T(2,128)S(1)} %stats.1), channel_id=1, replica_groups=mesh['vocab'=8,'chip'=2,'core'=2] {'vocab','chip'}, dimensions={0} | all-to-all | bytes 32768 | tf_op jit(solution)/shard_map/all_to_all | solution.py:182
  48.9 0.7 %loss.1 = (f32[2,4]{1,0:T(2,128)}, f32[1,1]{1,0:T(1,128)}) custom-call(f32[16,2,128]{2,1,0:T(2,128)S(1)} %all_to_all.5.received), custom_call_target="tpu_custom_call" | custom-call | tf_op jit(solution)/shard_map/loss/pallas_call | solution.py:183
  49.6 0.0 collective-permute-start.9
  49.6 1.3 %collective-permute-done.9 = f32[1,1]{1,0:T(1,128)} collective-permute-done((f32[1,1]{1,0:T(1,128)}, f32[1,1]{1,0:T(1,128)}, u32[]{:S(2)}, u32[]{:S(2)}) %collective-permute-start.9) | collective-permute-done | bytes 36 | tf_op jit(solution)/shard_map/ppermute | solution.py:34
  (8 shorter events, 0.1 us)
Async XLA Ops:
  1.6 8.1 %collective-permute-start.4 = (bf16[8,4736]{1,0:T(8,128)(2,1)S(1)}, bf16[8,4736]{1,0:T(8,128)(2,1)S(1)}, u32[]{:S(2)}, u32[]{:S(2)}) collective-permute-start(bf16[8,4736]{1,0:T(8,128)(2,1)S(1)} %slice.9), channel_id=1, source_target_pairs={{0,16},{1,9},{2,18},{3,11},{4,20},{5,13},{6,22},{7,15},{8,24},{9,1... | collective-permute-start | bytes 227336 | tf_op jit(solution)/shard_map/ppermute | solution.py:29
  5.7 4.0 %collective-permute-start = (bf16[8,2432]{1,0:T(8,128)(2,1)S(1)}, bf16[8,2432]{1,0:T(8,128)(2,1)S(1)}, u32[]{:S(2)}, u32[]{:S(2)}) collective-permute-start(bf16[8,2432]{1,0:T(8,128)(2,1)S(1)} %slice.8), channel_id=1, source_target_pairs={{0,2},{1,5},{2,0},{3,7},{4,6},{5,1},{6,4},{7,3},{8,10},{9,13},{10,... | collective-permute-start | bytes 116744 | tf_op jit(solution)/shard_map/ppermute | solution.py:29
  9.7 16.9 %collective-permute-start.7 = (bf16[7168,256]{1,0:T(8,128)(2,1)}, bf16[7168,256]{1,0:T(8,128)(2,1)}, u32[]{:S(2)}, u32[]{:S(2)}) collective-permute-start(bf16[7168,256]{1,0:T(8,128)(2,1)} %own.5), channel_id=1, source_target_pairs={{0,1},{1,0},{2,3},{3,2},{4,5},{5,4},{6,7},{7,6},{8,9},{9,8},{10,11... | collective-permute-start | bytes 11010056 | tf_op jit(solution)/shard_map/ppermute | solution.py:34
  9.7 6.9 %collective-permute-start.5 = (bf16[16,4736]{1,0:T(8,128)(2,1)S(1)}, bf16[16,4736]{1,0:T(8,128)(2,1)S(1)}, u32[]{:S(2)}, u32[]{:S(2)}) collective-permute-start(bf16[16,4736]{1,0:T(8,128)(2,1)S(1)} %pad_maximum_fusion.4), channel_id=1, source_target_pairs={{0,8},{1,17},{2,10},{3,19},{4,12},{5,21},{6,14},{7,23},{8,0},{9,25... | collective-permute-start | bytes 454664 | tf_op jit(solution)/shard_map/ppermute | solution.py:29
  11.4 6.8 %collective-permute-start.1 = (bf16[16,2432]{1,0:T(8,128)(2,1)S(1)}, bf16[16,2432]{1,0:T(8,128)(2,1)S(1)}, u32[]{:S(2)}, u32[]{:S(2)}) collective-permute-start(bf16[16,2432]{1,0:T(8,128)(2,1)S(1)} %pad_maximum_fusion.5), channel_id=1, source_target_pairs={{0,4},{1,3},{2,6},{3,1},{4,0},{5,7},{6,2},{7,5},{8,12},{9,11},{10,... | collective-permute-start | bytes 233480 | tf_op jit(solution)/shard_map/ppermute | solution.py:29
  16.6 9.6 %copy-start.2 = (s32[2,128]{1,0:T(2,128)S(1)}, s32[2,128]{1,0:T(2,128)}, u32[]{:S(2)}) copy-start(s32[2,128]{1,0:T(2,128)} %param.5) | copy-start | bytes 3076
  16.6 6.9 %collective-permute-start.6 = (bf16[32,4736]{1,0:T(8,128)(2,1)S(1)}, bf16[32,4736]{1,0:T(8,128)(2,1)S(1)}, u32[]{:S(2)}, u32[]{:S(2)}) collective-permute-start(bf16[32,4736]{1,0:T(8,128)(2,1)S(1)} %pad_maximum_fusion.2), channel_id=1, source_target_pairs={{0,2},{1,5},{2,0},{3,7},{4,6},{5,1},{6,4},{7,3},{8,10},{9,13},{10,... | collective-permute-start | bytes 909320 | tf_op jit(solution)/shard_map/ppermute | solution.py:29
  18.2 7.9 %collective-permute-start.2 = (bf16[32,2432]{1,0:T(8,128)(2,1)S(1)}, bf16[32,2432]{1,0:T(8,128)(2,1)S(1)}, u32[]{:S(2)}, u32[]{:S(2)}) collective-permute-start(bf16[32,2432]{1,0:T(8,128)(2,1)S(1)} %pad_maximum_fusion.3), channel_id=1, source_target_pairs={{0,16},{1,9},{2,18},{3,11},{4,20},{5,13},{6,22},{7,15},{8,24},{9,1... | collective-permute-start | bytes 466952 | tf_op jit(solution)/shard_map/ppermute | solution.py:29
  23.6 10.1 %collective-permute-start.8 = (bf16[64,4736]{1,0:T(8,128)(2,1)S(1)}, bf16[64,4736]{1,0:T(8,128)(2,1)S(1)}, u32[]{:S(2)}, u32[]{:S(2)}) collective-permute-start(bf16[64,4736]{1,0:T(8,128)(2,1)S(1)} %pad_maximum_fusion.kept_a), channel_id=1, source_target_pairs={{0,4},{1,3},{2,6},{3,1},{4,0},{5,7},{6,2},{7,5},{8,12},{9,11},{10,... | collective-permute-start | bytes 1818632 | tf_op jit(solution)/shard_map/ppermute | solution.py:29
  26.1 8.7 %collective-permute-start.3 = (bf16[64,2432]{1,0:T(8,128)(2,1)S(1)}, bf16[64,2432]{1,0:T(8,128)(2,1)S(1)}, u32[]{:S(2)}, u32[]{:S(2)}) collective-permute-start(bf16[64,2432]{1,0:T(8,128)(2,1)S(1)} %pad_maximum_fusion.1.kept_b), channel_id=1, source_target_pairs={{0,8},{1,17},{2,10},{3,19},{4,12},{5,21},{6,14},{7,23},{8,0},{9,25... | collective-permute-start | bytes 933896 | tf_op jit(solution)/shard_map/ppermute | solution.py:29
  26.6 2.0 %copy-start = (bf16[7168,256]{1,0:T(8,128)(2,1)S(1)}, bf16[7168,256]{1,0:T(8,128)(2,1)}, u32[]{:S(2)}) copy-start(bf16[7168,256]{1,0:T(8,128)(2,1)} %own.5) | copy-start | bytes 11010052
  28.7 5.0 %copy-start.1 = (bf16[7168,256]{1,0:T(8,128)(2,1)S(1)}, bf16[7168,256]{1,0:T(8,128)(2,1)}, u32[]{:S(2)}) copy-start(bf16[7168,256]{1,0:T(8,128)(2,1)} %own.5) | copy-start | bytes 11010052
  49.6 1.3 %collective-permute-start.9 = (f32[1,1]{1,0:T(1,128)}, f32[1,1]{1,0:T(1,128)}, u32[]{:S(2)}, u32[]{:S(2)}) collective-permute-start(f32[1,1]{1,0:T(1,128)} %get-tuple-element.11), channel_id=1, source_target_pairs={{0,1},{1,0},{2,3},{3,2},{4,5},{5,4},{6,7},{7,6},{8,9},{9,8},{10,11... | collective-permute-start | bytes 20 | tf_op jit(solution)/shard_map/ppermute | solution.py:34

commit v4 on v3

--- a/solution.py
+++ b/solution.py
@@ -57,21 +57,30 @@
         logits[target] = logits[target] + product[number * block : (number + 1) * block]
 
 
-def kept_kernel(flows, block, n_chip, kept_a, kept_b, own, other, other_out, logits, arrivals):
-    cut, depth = kept_a.shape[1], own.shape[0]
-    flow_rows = ((kept_a, 0), (kept_b, cut))
-    copies = []
-    for number, (first, count) in enumerate(((0, cut), (cut, depth - cut))):
-        span = pl.ds(first, count)
-        copies.append(pltpu.make_async_copy(other.at[span], other_out.at[span], arrivals.at[number]))
-    for copy in copies:
-        copy.start()
+def load_kernel(source, target, arrival):
+    copy = pltpu.make_async_copy(source, target, arrival)
+    copy.start()
+    copy.wait()
+
+
+def join_kernel(kept, arrived, out):
+    half = kept.shape[0]
+    out[:half] = kept[...]
+    out[half:] = arrived[...]
+
+
+def kept_kernel(flows, block, n_chip, targets, kept_a, kept_b, own, other, logits, wanted):
+    rows, tokens = wanted.shape[0], targets.shape[1]
+    tok_rows = block // targets.shape[0]
+    row = lax.broadcasted_iota(jnp.int32, (rows, tokens), 0)
+    token = (2 * (row // block) + lax.axis_index("core")) * tok_rows + row % tok_rows
+    ids = jnp.where(row // tok_rows % 2 == 0, targets[0:1, :], targets[1:2, :])
+    here = token == lax.broadcasted_iota(jnp.int32, (rows, tokens), 1)
+    wanted[...] = jnp.broadcast_to(jnp.sum(jnp.where(here, ids, 0), axis=1, keepdims=True), wanted.shape)
     logits[...] = jnp.zeros_like(logits)
-    for number, (kept, first) in enumerate(flow_rows):
-        add_products(flows[number], block, 0, n_chip, kept, own, 0, first, logits)
-    for number, (kept, first) in enumerate(flow_rows):
-        copies[number].wait()
-        add_products(flows[number], block, 0, n_chip, kept, other_out, 1, first, logits)
+    for number, (kept, first) in enumerate(((kept_a, 0), (kept_b, kept_a.shape[1]))):
+        for side, columns in enumerate((own, other)):
+            add_products(flows[number], block, 0, n_chip, kept, columns, side, first, logits)
 
 
 def first_kernel(flows, block, n_chip, arrived, own, other, partial, logits):
@@ -93,7 +102,7 @@
     device = 2 * chip + core
     lane = lax.broadcasted_iota(jnp.int32, values.shape, 1)
     column_ids = jnp.where(lane < width, device * width + lane, (device ^ 1) * width + lane - width)
-    picked = jnp.sum(jnp.where(column_ids == wanted[...], values, 0.0), axis=1, keepdims=True)
+    picked = jnp.sum(jnp.where(column_ids == wanted[:, :1], values, 0.0), axis=1, keepdims=True)
     member = lax.broadcasted_iota(jnp.int32, (values.shape[0], 128), 1)
     table = jnp.where(member == 0, highest + jnp.log(exp_total), picked)
     sent = jnp.transpose(table)[:2]
@@ -111,11 +120,34 @@
     loss = highest + jnp.log(exp_total) - picked
     lane = lax.broadcasted_iota(jnp.int32, loss.shape, 1)
     weight = jnp.where(lane // tok_rows % 2 == 0, 1.0 / rows, MTP_WEIGHT / rows)
-    part[...] = jnp.sum(loss * weight, axis=1, keepdims=True)
+    part[...] = jnp.broadcast_to(jnp.sum(loss * weight, axis=1, keepdims=True), part.shape)
     repeated = jnp.broadcast_to(loss, (8, rows))
     for head in range(2):
         turned = pltpu.roll(repeated, rows - chip * block - head * tok_rows, 1)
         own_loss[pl.ds(head, 1), :] = turned[:1, :tok_rows]
+
+
+def load(columns):
+    return pl.pallas_call(
+        load_kernel,
+        out_shape=jax.ShapeDtypeStruct(columns.shape, columns.dtype),
+        in_specs=[pl.BlockSpec(memory_space=pltpu.HBM)],
+        out_specs=pl.BlockSpec(memory_space=pltpu.VMEM),
+        scratch_shapes=[pltpu.SemaphoreType.DMA],
+        cost_estimate=pl.CostEstimate(flops=0, bytes_accessed=4 * columns.size, transcendentals=0),
+        compiler_params=pltpu.CompilerParams(vmem_limit_bytes=2**20 + 2 * columns.size),
+    )(columns)
+
+
+def join(kept, arrived):
+    rows, depth = kept.shape
+    return pl.pallas_call(
+        join_kernel,
+        out_shape=jax.ShapeDtypeStruct((2 * rows, depth), kept.dtype),
+        cost_estimate=pl.CostEstimate(flops=0, bytes_accessed=8 * kept.size, transcendentals=0),
+        compiler_params=pltpu.CompilerParams(vmem_limit_bytes=2**20 + 8 * kept.size),
+        name="join",
+    )(kept, arrived)
 
 
 def local(hidden, unembed, targets):
@@ -125,9 +157,9 @@
     n_vocab, n_chip = lax.axis_size("vocab"), lax.axis_size("chip")
     n_chips = n_vocab * n_chip
     flows = gather_orders(n_vocab, n_chip)
-    core = lax.axis_index("core")
     rows = n_chips * block
 
+    other_columns = to_other_core(unembed, n_chips)
     cut = depth // 128 * 2 // 3 * 128
     own_rows = hidden.reshape(block, depth)
     kept = [own_rows[:, :cut], own_rows[:, cut:]]
@@ -137,40 +169,30 @@
         for flow in range(2):
             masks = (flows[flow][0][number], flows[flow][1][number])
             arrived[flow] = exchange(kept[flow], masks, n_chips)
-        if number == 0:
-            later_columns, _ = lax.optimization_barrier((unembed, arrived))
-            other_columns = to_other_core(later_columns, n_chips)
         if number < stages - 1:
             for flow in range(2):
-                kept[flow] = jnp.concatenate([kept[flow], arrived[flow]], axis=0)
-    mine = lax.dynamic_index_in_dim(targets.reshape(heads, n_chips, 2, tok_rows), core, 2, keepdims=False)
-    wanted = jnp.transpose(mine, (1, 0, 2)).reshape(rows, 1)
+                kept[flow] = join(kept[flow], arrived[flow])
+    own_near, other_near = unembed, load(other_columns)
     cost = pl.CostEstimate(
         flops=2 * rows * width * depth, bytes_accessed=(rows + 4 * width) * depth, transcendentals=0
     )
-    held = 2 * (rows + 2 * width) * depth + 4 * rows * (8 * width + 2 * 128 + 8 * n_chips)
+    held = 2 * (rows + 2 * width) * depth + 4 * rows * (8 * width + 3 * rows + 8 * n_chips)
     params = pltpu.CompilerParams(vmem_limit_bytes=held + 2**21)
-    in_vmem = pl.BlockSpec(memory_space=pltpu.VMEM)
-    in_hbm = pl.BlockSpec(memory_space=pltpu.HBM)
-    columns = jax.ShapeDtypeStruct(unembed.shape, unembed.dtype)
-    other_near, partial = pl.pallas_call(
+    logits = jax.ShapeDtypeStruct((rows, 2 * width), jnp.float32)
+    partial, wanted = pl.pallas_call(
         functools.partial(kept_kernel, flows, block, n_chip),
-        out_shape=(columns, jax.ShapeDtypeStruct((rows, 2 * width), jnp.float32)),
-        in_specs=[in_vmem, in_vmem, in_vmem, in_hbm],
-        out_specs=(in_vmem, in_vmem),
-        scratch_shapes=[pltpu.SemaphoreType.DMA((2,))],
+        out_shape=(logits, jax.ShapeDtypeStruct((rows, 128), jnp.int32)),
         cost_estimate=cost,
         compiler_params=params,
         name="kept",
-    )(kept[0], kept[1], unembed, other_columns)
-    logits = jax.ShapeDtypeStruct((rows, 2 * width), jnp.float32)
+    )(targets, kept[0], kept[1], own_near, other_near)
     partial = pl.pallas_call(
         functools.partial(first_kernel, flows, block, n_chip),
         out_shape=logits,
         cost_estimate=cost,
         compiler_params=params,
         name="first",
-    )(arrived[0], unembed, other_near, partial)
+    )(arrived[0], own_near, other_near, partial)
     sent = pl.pallas_call(
         functools.partial(stats_kernel, flows, block, n_chip),
         out_shape=jax.ShapeDtypeStruct((n_chips, 2, rows), jnp.float32),
@@ -178,15 +200,15 @@
         cost_estimate=cost,
         compiler_params=params,
         name="stats",
-    )(wanted, arrived[1], unembed, other_near, partial)
+    )(wanted, arrived[1], own_near, other_near, partial)
     received = lax.all_to_all(sent, CHIPS, split_axis=0, concat_axis=0, tiled=True)
     token_loss, part = pl.pallas_call(
         functools.partial(loss_kernel, n_chip, block, tok_rows),
-        out_shape=(jax.ShapeDtypeStruct((heads, tok_rows), jnp.float32), jax.ShapeDtypeStruct((1, 1), jnp.float32)),
+        out_shape=(jax.ShapeDtypeStruct((heads, tok_rows), jnp.float32), jax.ShapeDtypeStruct((8, 128), jnp.float32)),
         compiler_params=pltpu.CompilerParams(vmem_limit_bytes=2**20 + 4 * 4 * n_chips * 8 * rows),
         name="loss",
     )(received)
-    total = (part + to_other_core(part, n_chips)).reshape(())
+    total = (part + to_other_core(part, n_chips))[0, 0]
     return token_loss, total
 
 

time: 53.5 us -> 69.6 us (1.30)
  waiting for transfers between devices: 13.6 us -> 29.9 us
  starting transfers between devices: 13.1 us -> 16.1 us
  between operations: 3.15 us -> 0.73 us
  local copies, waits for them, and re-layouts: 3.4 us -> 1.47 us
  blocking collectives: 13.3 us -> 15 us
    ppermute x8, waiting for transfers between devices: 12.4 us -> 28.7 us  [exchange(): return lax.ppermute(value, AXES, pairs)]
    pallas_call x1, Pallas kernels: 4.06 us -> 1.45 us  [local(): pl.pallas_call(functools.partial(kept_kernel, flows, block, n_chip), out_...]
    ppermute x8, starting transfers between devices: 13.1 us -> 15.6 us  [exchange(): return lax.ppermute(value, AXES, pairs)]
    pallas_call x0 -> x7, Pallas kernels: none -> 2.16 us  [the longest x1 2.05 us: load(): pl.pallas_call(load_kernel, out_shape=jax.ShapeDtypeStruct(columns.shape,...]
    unnamed x6 -> x4, local copies, waits for them, and re-layouts: 2.04 us -> 0.01 us
    all_to_all x1, blocking collectives: 13.3 us -> 15 us  [local(): lax.all_to_all(sent, CHIPS, split_axis=0, concat_axis=0, tiled=True)]
  transfers between devices with their start and end apart: 10 -> 10, of which waited for: 7 -> 8; matrix products, arithmetic and copies ran while one was open for 1% -> 1% of each run, Pallas kernels for 9% -> 7%
where the time goes in v4:
time: 69.6 us; the launch traced here: 69.4 us
  waiting for transfers between devices  29.9 us (43%)
  starting transfers between devices  16.1 us (23%)
  blocking collectives  15 us (22%)
  Pallas kernels  6.11 us (9%)
  local copies, waits for them, and re-layouts  1.47 us (2%)
  between operations  0.73 us (1%)
    ppermute x8, waiting for transfers between devices, exchange(): return lax.ppermute(value, AXES, pairs)  28.7 us
    ppermute x8, starting transfers between devices, exchange(): return lax.ppermute(value, AXES, pairs)  15.6 us
    all_to_all x1, blocking collectives, local(): lax.all_to_all(sent, CHIPS, split_axis=0, concat_axis=0, tiled=True)  15 us
    pallas_call x1, Pallas kernels, load(): pl.pallas_call(load_kernel, out_shape=jax.ShapeDtypeStruct(columns.shape,...  2.05 us
    pallas_call x1, Pallas kernels, local(): pl.pallas_call(functools.partial(kept_kernel, flows, block, n_chip), out_...  1.45 us
  transfers between devices with their start and end apart: 10, of which 8 were waited for; matrix products, arithmetic and copies ran while one was open for 1% of the time, Pallas kernels for 7%

profile of v4, /device:TPU:0, one launch (start us, length us, event | category | flops | bytes accessed | tf_op | source)
XLA Modules:
  0.0 69.4 jit_solution(5188641913752524445)
XLA Ops:
  0.6 0.6 collective-permute-start.6
  1.2 0.9 %reshape.7 = bf16[8,7168]{1,0:T(8,128)(2,1)S(1)} reshape(bf16[2,4,7168]{2,1,0:T(4,128)(2,1)} %param.3) | data formatting | bytes 229376 | tf_op jit(solution)/shard_map/reshape | solution.py:164
  2.1 3.7 %collective-permute-start = (bf16[8,4736]{1,0:T(8,128)(2,1)S(1)}, bf16[8,4736]{1,0:T(8,128)(2,1)S(1)}, u32[]{:S(2)}, u32[]{:S(2)}) collective-permute-start(bf16[8,4736]{1,0:T(8,128)(2,1)S(1)} %slice.12.kept), channel_id=1, source_target_pairs={{0,16},{1,9},{2,18},{3,11},{4,20},{5,13},{6,22},{7,15},{8,24},{9,1... | collective-permute-start | bytes 227336 | tf_op jit(solution)/shard_map/ppermute | solution.py:29
  5.8 2.4 %collective-permute-done.arrived = bf16[8,4736]{1,0:T(8,128)(2,1)S(1)} collective-permute-done((bf16[8,4736]{1,0:T(8,128)(2,1)S(1)}, bf16[8,4736]{1,0:T(8,128)(2,1)S(1)}, u32[]{:S(2)}, u32[]{:S(2)}) %collective-permute-start) | collective-permute-done | bytes 75808 | tf_op jit(solution)/shard_map/ppermute | solution.py:29
  8.2 2.4 %collective-permute-start.1 = (bf16[16,4736]{1,0:T(8,128)(2,1)S(1)}, bf16[16,4736]{1,0:T(8,128)(2,1)S(1)}, u32[]{:S(2)}, u32[]{:S(2)}) collective-permute-start(bf16[16,4736]{1,0:T(8,128)(2,1)S(1)} %join.6.kept), channel_id=1, source_target_pairs={{0,8},{1,17},{2,10},{3,19},{4,12},{5,21},{6,14},{7,23},{8,0},{9,25... | collective-permute-start | bytes 454664 | tf_op jit(solution)/shard_map/ppermute | solution.py:29
  10.6 4.1 %collective-permute-done.1.arrived = bf16[16,4736]{1,0:T(8,128)(2,1)S(1)} collective-permute-done((bf16[16,4736]{1,0:T(8,128)(2,1)S(1)}, bf16[16,4736]{1,0:T(8,128)(2,1)S(1)}, u32[]{:S(2)}, u32[]{:S(2)}) %collective-permute-start.1) | collective-permute-done | bytes 151584 | tf_op jit(solution)/shard_map/ppermute | solution.py:29
  14.7 1.6 %collective-permute-start.2 = (bf16[32,4736]{1,0:T(8,128)(2,1)S(1)}, bf16[32,4736]{1,0:T(8,128)(2,1)S(1)}, u32[]{:S(2)}, u32[]{:S(2)}) collective-permute-start(bf16[32,4736]{1,0:T(8,128)(2,1)S(1)} %join.7.kept), channel_id=1, source_target_pairs={{0,2},{1,5},{2,0},{3,7},{4,6},{5,1},{6,4},{7,3},{8,10},{9,13},{10,... | collective-permute-start | bytes 909320 | tf_op jit(solution)/shard_map/ppermute | solution.py:29
  16.2 5.3 %collective-permute-done.2.arrived = bf16[32,4736]{1,0:T(8,128)(2,1)S(1)} collective-permute-done((bf16[32,4736]{1,0:T(8,128)(2,1)S(1)}, bf16[32,4736]{1,0:T(8,128)(2,1)S(1)}, u32[]{:S(2)}, u32[]{:S(2)}) %collective-permute-start.2) | collective-permute-done | bytes 303136 | tf_op jit(solution)/shard_map/ppermute | solution.py:29
  21.6 1.6 %collective-permute-start.8 = (bf16[64,4736]{1,0:T(8,128)(2,1)S(1)}, bf16[64,4736]{1,0:T(8,128)(2,1)S(1)}, u32[]{:S(2)}, u32[]{:S(2)}) collective-permute-start(bf16[64,4736]{1,0:T(8,128)(2,1)S(1)} %join.8.kept_a), channel_id=1, source_target_pairs={{0,4},{1,3},{2,6},{3,1},{4,0},{5,7},{6,2},{7,5},{8,12},{9,11},{10,... | collective-permute-start | bytes 1818632 | tf_op jit(solution)/shard_map/ppermute | solution.py:29
  23.2 1.5 %collective-permute-start.3 = (bf16[8,2432]{1,0:T(8,128)(2,1)S(1)}, bf16[8,2432]{1,0:T(8,128)(2,1)S(1)}, u32[]{:S(2)}, u32[]{:S(2)}) collective-permute-start(bf16[8,2432]{1,0:T(8,128)(2,1)S(1)} %slice.13.kept), channel_id=1, source_target_pairs={{0,2},{1,5},{2,0},{3,7},{4,6},{5,1},{6,4},{7,3},{8,10},{9,13},{10,... | collective-permute-start | bytes 116744 | tf_op jit(solution)/shard_map/ppermute | solution.py:29
  24.7 2.9 %collective-permute-done.3.arrived = bf16[8,2432]{1,0:T(8,128)(2,1)S(1)} collective-permute-done((bf16[8,2432]{1,0:T(8,128)(2,1)S(1)}, bf16[8,2432]{1,0:T(8,128)(2,1)S(1)}, u32[]{:S(2)}, u32[]{:S(2)}) %collective-permute-start.3) | collective-permute-done | bytes 38944 | tf_op jit(solution)/shard_map/ppermute | solution.py:29
  27.6 0.5 collective-permute-start.4
  28.1 4.5 %collective-permute-done.4.arrived = bf16[16,2432]{1,0:T(8,128)(2,1)S(1)} collective-permute-done((bf16[16,2432]{1,0:T(8,128)(2,1)S(1)}, bf16[16,2432]{1,0:T(8,128)(2,1)S(1)}, u32[]{:S(2)}, u32[]{:S(2)}) %collective-permute-start.4) | collective-permute-done | bytes 77856 | tf_op jit(solution)/shard_map/ppermute | solution.py:29
  32.6 2.5 %collective-permute-start.5 = (bf16[32,2432]{1,0:T(8,128)(2,1)S(1)}, bf16[32,2432]{1,0:T(8,128)(2,1)S(1)}, u32[]{:S(2)}, u32[]{:S(2)}) collective-permute-start(bf16[32,2432]{1,0:T(8,128)(2,1)S(1)} %join.10.kept), channel_id=1, source_target_pairs={{0,16},{1,9},{2,18},{3,11},{4,20},{5,13},{6,22},{7,15},{8,24},{9,1... | collective-permute-start | bytes 466952 | tf_op jit(solution)/shard_map/ppermute | solution.py:29
  35.1 9.0 %collective-permute-done.5.arrived = bf16[32,2432]{1,0:T(8,128)(2,1)S(1)} collective-permute-done((bf16[32,2432]{1,0:T(8,128)(2,1)S(1)}, bf16[32,2432]{1,0:T(8,128)(2,1)S(1)}, u32[]{:S(2)}, u32[]{:S(2)}) %collective-permute-start.5) | collective-permute-done | bytes 155680 | tf_op jit(solution)/shard_map/ppermute | solution.py:29
  44.1 0.0 copy-start
  44.1 0.0 copy-start.1
  44.1 1.9 %collective-permute-start.7 = (bf16[64,2432]{1,0:T(8,128)(2,1)S(1)}, bf16[64,2432]{1,0:T(8,128)(2,1)S(1)}, u32[]{:S(2)}, u32[]{:S(2)}) collective-permute-start(bf16[64,2432]{1,0:T(8,128)(2,1)S(1)} %join.11.kept_b), channel_id=1, source_target_pairs={{0,8},{1,17},{2,10},{3,19},{4,12},{5,21},{6,14},{7,23},{8,0},{9,25... | collective-permute-start | bytes 933896 | tf_op jit(solution)/shard_map/ppermute | solution.py:29
  46.0 0.0 collective-permute-done.6.source
  46.0 2.0 %shard_map.50.other = bf16[7168,256]{1,0:T(8,128)(2,1)S(1)} custom-call(bf16[7168,256]{1,0:T(8,128)(2,1)} %collective-permute-done.6.source), custom_call_target="tpu_custom_call" | custom-call | bytes 7340032 | tf_op jit(solution)/shard_map/pallas_call | solution.py:131
  48.1 0.0 copy-done
  48.1 0.0 copy-done.1
  48.1 1.4 %kept.1 = (f32[128,512]{1,0:T(8,128)S(1)}, s32[128,128]{1,0:T(8,128)S(1)}) custom-call(s32[2,128]{1,0:T(2,128)S(1)} %copy-done.1, bf16[64,4736]{1,0:T(8,128)(2,1)S(1)} %join.8.kept_a, bf16[64,2432]{1,0:T(8,128)(2,1)S(1)} %join.11.kept_b, bf16[7168,256]{1,0:T(8,128)(2,1)S(1)} %copy-done, bf16[7168,256]{1,0:T(8,128)(2,1)S(1)} %shard_map.50.other), custom_call_target="tpu_custom_call" | custom-call | flops 469762048 | bytes 8257536 | tf_op jit(solution)/shard_map/kept/pallas_call | solution.py:182
  49.6 0.0 collective-permute-done.8.arrived
  49.6 1.0 %first.1.partial = f32[128,512]{1,0:T(8,128)S(1)} custom-call(bf16[64,4736]{1,0:T(8,128)(2,1)S(1)} %collective-permute-done.8.arrived, bf16[7168,256]{1,0:T(8,128)(2,1)S(1)} %copy-done, bf16[7168,256]{1,0:T(8,128)(2,1)S(1)} %shard_map.50.other, f32[128,512]{1,0:T(8,128)S(1)} %get-tuple-element.7.partial), custom_call_target="tpu_custom_call" | custom-call | flops 469762048 | bytes 8257536 | tf_op jit(solution)/shard_map/first/pallas_call | solution.py:189
  50.6 0.5 collective-permute-done.7.arrived
  51.1 0.8 %stats.1 = f32[16,2,128]{2,1,0:T(2,128)S(1)} custom-call(s32[128,128]{1,0:T(8,128)S(1)} %get-tuple-element.6.wanted, bf16[64,2432]{1,0:T(8,128)(2,1)S(1)} %collective-permute-done.7.arrived, bf16[7168,256]{1,0:T(8,128)(2,1)S(1)} %copy-done, bf16[7168,256]{1,0:T(8,128)(2,1)S(1)} %shard_map.50.other, f32[128,512]{1,0:T(8,128)S(1)} %first.1.partial), custom_call_target="tpu_custom_call" | custom-call | flops 469762048 | bytes 8257536 | tf_op jit(solution)/shard_map/stats/pallas_call | solution.py:196
  52.0 15.0 %all_to_all.5.received = f32[16,2,128]{2,1,0:T(2,128)S(1)} all-to-all(f32[16,2,128]{2,1,0:T(2,128)S(1)} %stats.1), channel_id=1, replica_groups=mesh['vocab'=8,'chip'=2,'core'=2] {'vocab','chip'}, dimensions={0} | all-to-all | bytes 32768 | tf_op jit(solution)/shard_map/all_to_all | solution.py:204
  67.0 0.7 loss.1
  67.7 0.0 collective-permute-start.9
  67.7 1.2 %collective-permute-done.9 = f32[8,128]{1,0:T(8,128)S(1)} collective-permute-done((f32[8,128]{1,0:T(8,128)S(1)}, f32[8,128]{1,0:T(8,128)S(1)}, u32[]{:S(2)}, u32[]{:S(2)}) %collective-permute-start.9) | collective-permute-done | bytes 4128 | tf_op jit(solution)/shard_map/ppermute | solution.py:34
  68.8 0.5 slice.11
  (9 shorter events, 0.1 us)
Async XLA Ops:
  0.6 45.4 %collective-permute-start.6 = (bf16[7168,256]{1,0:T(8,128)(2,1)}, bf16[7168,256]{1,0:T(8,128)(2,1)}, u32[]{:S(2)}, u32[]{:S(2)}) collective-permute-start(bf16[7168,256]{1,0:T(8,128)(2,1)} %own.5), channel_id=1, source_target_pairs={{0,1},{1,0},{2,3},{3,2},{4,5},{5,4},{6,7},{7,6},{8,9},{9,8},{10,11... | collective-permute-start | bytes 11010056 | tf_op jit(solution)/shard_map/ppermute | solution.py:34
  2.1 6.0 %collective-permute-start = (bf16[8,4736]{1,0:T(8,128)(2,1)S(1)}, bf16[8,4736]{1,0:T(8,128)(2,1)S(1)}, u32[]{:S(2)}, u32[]{:S(2)}) collective-permute-start(bf16[8,4736]{1,0:T(8,128)(2,1)S(1)} %slice.12.kept), channel_id=1, source_target_pairs={{0,16},{1,9},{2,18},{3,11},{4,20},{5,13},{6,22},{7,15},{8,24},{9,1... | collective-permute-start | bytes 227336 | tf_op jit(solution)/shard_map/ppermute | solution.py:29
  8.2 6.5 %collective-permute-start.1 = (bf16[16,4736]{1,0:T(8,128)(2,1)S(1)}, bf16[16,4736]{1,0:T(8,128)(2,1)S(1)}, u32[]{:S(2)}, u32[]{:S(2)}) collective-permute-start(bf16[16,4736]{1,0:T(8,128)(2,1)S(1)} %join.6.kept), channel_id=1, source_target_pairs={{0,8},{1,17},{2,10},{3,19},{4,12},{5,21},{6,14},{7,23},{8,0},{9,25... | collective-permute-start | bytes 454664 | tf_op jit(solution)/shard_map/ppermute | solution.py:29
  14.7 6.9 %collective-permute-start.2 = (bf16[32,4736]{1,0:T(8,128)(2,1)S(1)}, bf16[32,4736]{1,0:T(8,128)(2,1)S(1)}, u32[]{:S(2)}, u32[]{:S(2)}) collective-permute-start(bf16[32,4736]{1,0:T(8,128)(2,1)S(1)} %join.7.kept), channel_id=1, source_target_pairs={{0,2},{1,5},{2,0},{3,7},{4,6},{5,1},{6,4},{7,3},{8,10},{9,13},{10,... | collective-permute-start | bytes 909320 | tf_op jit(solution)/shard_map/ppermute | solution.py:29
  21.6 28.0 %collective-permute-start.8 = (bf16[64,4736]{1,0:T(8,128)(2,1)S(1)}, bf16[64,4736]{1,0:T(8,128)(2,1)S(1)}, u32[]{:S(2)}, u32[]{:S(2)}) collective-permute-start(bf16[64,4736]{1,0:T(8,128)(2,1)S(1)} %join.8.kept_a), channel_id=1, source_target_pairs={{0,4},{1,3},{2,6},{3,1},{4,0},{5,7},{6,2},{7,5},{8,12},{9,11},{10,... | collective-permute-start | bytes 1818632 | tf_op jit(solution)/shard_map/ppermute | solution.py:29
  23.2 4.4 %collective-permute-start.3 = (bf16[8,2432]{1,0:T(8,128)(2,1)S(1)}, bf16[8,2432]{1,0:T(8,128)(2,1)S(1)}, u32[]{:S(2)}, u32[]{:S(2)}) collective-permute-start(bf16[8,2432]{1,0:T(8,128)(2,1)S(1)} %slice.13.kept), channel_id=1, source_target_pairs={{0,2},{1,5},{2,0},{3,7},{4,6},{5,1},{6,4},{7,3},{8,10},{9,13},{10,... | collective-permute-start | bytes 116744 | tf_op jit(solution)/shard_map/ppermute | solution.py:29
  27.6 5.0 %collective-permute-start.4 = (bf16[16,2432]{1,0:T(8,128)(2,1)S(1)}, bf16[16,2432]{1,0:T(8,128)(2,1)S(1)}, u32[]{:S(2)}, u32[]{:S(2)}) collective-permute-start(bf16[16,2432]{1,0:T(8,128)(2,1)S(1)} %join.9.kept), channel_id=1, source_target_pairs={{0,4},{1,3},{2,6},{3,1},{4,0},{5,7},{6,2},{7,5},{8,12},{9,11},{10,... | collective-permute-start | bytes 233480 | tf_op jit(solution)/shard_map/ppermute | solution.py:29
  32.6 11.5 %collective-permute-start.5 = (bf16[32,2432]{1,0:T(8,128)(2,1)S(1)}, bf16[32,2432]{1,0:T(8,128)(2,1)S(1)}, u32[]{:S(2)}, u32[]{:S(2)}) collective-permute-start(bf16[32,2432]{1,0:T(8,128)(2,1)S(1)} %join.10.kept), channel_id=1, source_target_pairs={{0,16},{1,9},{2,18},{3,11},{4,20},{5,13},{6,22},{7,15},{8,24},{9,1... | collective-permute-start | bytes 466952 | tf_op jit(solution)/shard_map/ppermute | solution.py:29
  44.1 4.0 %copy-start = (bf16[7168,256]{1,0:T(8,128)(2,1)S(1)}, bf16[7168,256]{1,0:T(8,128)(2,1)}, u32[]{:S(2)}) copy-start(bf16[7168,256]{1,0:T(8,128)(2,1)} %own.5) | copy-start | bytes 11010052
  44.1 4.0 %copy-start.1 = (s32[2,128]{1,0:T(2,128)S(1)}, s32[2,128]{1,0:T(2,128)}, u32[]{:S(2)}) copy-start(s32[2,128]{1,0:T(2,128)} %targets.1) | copy-start | bytes 3076
  44.1 7.0 %collective-permute-start.7 = (bf16[64,2432]{1,0:T(8,128)(2,1)S(1)}, bf16[64,2432]{1,0:T(8,128)(2,1)S(1)}, u32[]{:S(2)}, u32[]{:S(2)}) collective-permute-start(bf16[64,2432]{1,0:T(8,128)(2,1)S(1)} %join.11.kept_b), channel_id=1, source_target_pairs={{0,8},{1,17},{2,10},{3,19},{4,12},{5,21},{6,14},{7,23},{8,0},{9,25... | collective-permute-start | bytes 933896 | tf_op jit(solution)/shard_map/ppermute | solution.py:29
  67.7 1.2 %collective-permute-start.9 = (f32[8,128]{1,0:T(8,128)S(1)}, f32[8,128]{1,0:T(8,128)S(1)}, u32[]{:S(2)}, u32[]{:S(2)}) collective-permute-start(f32[8,128]{1,0:T(8,128)S(1)} %get-tuple-element.9), channel_id=1, source_target_pairs={{0,1},{1,0},{2,3},{3,2},{4,5},{5,4},{6,7},{7,6},{8,9},{9,8},{10,11... | collective-permute-start | bytes 12296 | tf_op jit(solution)/shard_map/ppermute | solution.py:34

commit v5 on v4

v5 whole, which is shorter than its diff:
```python
import functools
import jax
import jax.numpy as jnp
from jax import lax
from jax.experimental import pallas as pl
from jax.experimental.pallas import tpu as pltpu
from jax.sharding import Mesh, PartitionSpec as P

MTP_WEIGHT = 0.3
AXIS = "device"


def bits(count):
    return [1 << place for place in range(count.bit_length() - 1)]


def gather_orders(n_vocab, n_chip):
    near = bits(n_chip) + [n_chip * mask for mask in bits(n_vocab)[:1]]
    far = [n_chip * mask for mask in bits(n_vocab)[1:]]
    return (
        (far[::-1] + near[::-1], far + near),
        (near + far[::-1], near[::-1] + far),
    )


def parity(chip, n_chips):
    odd = chip
    for place in range(1, n_chips.bit_length() - 1):
        odd = odd ^ (chip >> place)
    return odd & 1


def team_devices(n_chips):
    return [[2 * chip + (team ^ parity(chip, n_chips)) for chip in range(n_chips)] for team in range(2)]


def place_of(n_chips):
    device = lax.axis_index(AXIS)
    chip, core = device // 2, device % 2
    return device, chip, core ^ parity(chip, n_chips)


def exchange(value, masks, n_chips):
    teams = team_devices(n_chips)
    pairs = [(teams[team][chip], teams[team][chip ^ masks[team]]) for team in range(2) for chip in range(n_chips)]
    return lax.ppermute(value, AXIS, sorted(pairs))


def to_other_core(value, n_chips):
    pairs = [(source, source ^ 1) for source in range(2 * n_chips)]
    return lax.ppermute(value, AXIS, pairs)


def offset(masks, place):
    total = 0
    for number, mask in enumerate(masks):
        if place >> number & 1:
            total ^= mask
    return total


def add_products(orders, block, part, n_chips, rows, columns, side, first_depth, logits):
    _, chip, team = place_of(n_chips)
    blocks, width = rows.shape[0] // block, columns.shape[1]
    product = jnp.dot(
        rows[...], columns[pl.ds(first_depth, rows.shape[1]), :], preferred_element_type=jnp.float32
    )
    for number in range(blocks):
        place = part * blocks + number
        shift = jnp.where(team == 0, offset(orders[0], place), offset(orders[1], place))
        first = pl.multiple_of((chip ^ shift) * block, block)
        target = (pl.ds(first, block), pl.ds(side * width, width))
        logits[target] = logits[target] + product[number * block : (number + 1) * block]


def load_kernel(source, target, arrival):
    copy = pltpu.make_async_copy(source, target, arrival)
    copy.start()
    copy.wait()


def join_kernel(kept, arrived, out):
    half = kept.shape[0]
    out[:half] = kept[...]
    out[half:] = arrived[...]


def kept_kernel(flows, block, n_chips, targets, kept_a, kept_b, own, other, logits, wanted):
    rows, tokens = wanted.shape[0], targets.shape[1]
    tok_rows = block // targets.shape[0]
    row = lax.broadcasted_iota(jnp.int32, (rows, tokens), 0)
    team = place_of(n_chips)[2]
    token = (2 * (row // block) + (team ^ parity(row // block, n_chips))) * tok_rows + row % tok_rows
    ids = jnp.where(row // tok_rows % 2 == 0, targets[0:1, :], targets[1:2, :])
    here = token == lax.broadcasted_iota(jnp.int32, (rows, tokens), 1)
    wanted[...] = jnp.broadcast_to(jnp.sum(jnp.where(here, ids, 0), axis=1, keepdims=True), wanted.shape)
    logits[...] = jnp.zeros_like(logits)
    for number, (kept, first) in enumerate(((kept_a, 0), (kept_b, kept_a.shape[1]))):
        for side, columns in enumerate((own, other)):
            add_products(flows[number], block, 0, n_chips, kept, columns, side, first, logits)


def first_kernel(flows, block, n_chips, arrived, own, other, partial, logits):
    logits[...] = partial[...]
    for side, columns in enumerate((own, other)):
        add_products(flows[0], block, 1, n_chips, arrived, columns, side, 0, logits)


def stats_kernel(flows, block, n_chips, wanted, arrived, own, other, partial, out, logits):
    device, _, _ = place_of(n_chips)
    width = own.shape[1]
    logits[...] = partial[...]
    for side, columns in enumerate((own, other)):
        add_products(flows[1], block, 1, n_chips, arrived, columns, side, own.shape[0] - arrived.shape[1], logits)
    values = logits[...]
    highest = jnp.max(values, axis=1, keepdims=True)
    exp_total = jnp.sum(jnp.exp(values - highest), axis=1, keepdims=True)
    lane = lax.broadcasted_iota(jnp.int32, values.shape, 1)
    column_ids = jnp.where(lane < width, device * width + lane, (device ^ 1) * width + lane - width)
    picked = jnp.sum(jnp.where(column_ids == wanted[:, :1], values, 0.0), axis=1, keepdims=True)
    member = lax.broadcasted_iota(jnp.int32, (values.shape[0], 128), 1)
    table = jnp.where(member == 0, highest + jnp.log(exp_total), picked)
    out[...] = jnp.transpose(table)[:2]


def pack_kernel(own, other, out):
    for chip_number in range(out.shape[0]):
        out[chip_number, :2] = own[...]
        out[chip_number, 2:] = other[...]


def loss_kernel(n_chips, block, tok_rows, received, own_loss, total):
    chip = place_of(n_chips)[1]
    rows = received.shape[2]
    lane = lax.broadcasted_iota(jnp.int32, (1, rows), 1)
    weight = jnp.where(lane // tok_rows % 2 == 0, 1.0 / rows, MTP_WEIGHT / rows)
    weighted = []
    for first in (2, 0):
        log_sums = received[:, first, :]
        highest = jnp.max(log_sums, axis=0, keepdims=True)
        exp_total = jnp.sum(jnp.exp(log_sums - highest), axis=0, keepdims=True)
        loss = highest + jnp.log(exp_total) - jnp.sum(received[:, first + 1, :], axis=0, keepdims=True)
        weighted.append(loss * weight)
    total[...] = jnp.sum(weighted[0] + weighted[1], axis=1, keepdims=True)
    repeated = jnp.broadcast_to(loss, (8, rows))
    for head in range(2):
        turned = pltpu.roll(repeated, rows - chip * block - head * tok_rows, 1)
        own_loss[pl.ds(head, 1), :] = turned[:1, :tok_rows]


def load(columns):
    return pl.pallas_call(
        load_kernel,
        out_shape=jax.ShapeDtypeStruct(columns.shape, columns.dtype),
        in_specs=[pl.BlockSpec(memory_space=pltpu.HBM)],
        out_specs=pl.BlockSpec(memory_space=pltpu.VMEM),
        scratch_shapes=[pltpu.SemaphoreType.DMA],
        cost_estimate=pl.CostEstimate(flops=0, bytes_accessed=4 * columns.size, transcendentals=0),
        compiler_params=pltpu.CompilerParams(vmem_limit_bytes=2**20 + 2 * columns.size),
    )(columns)


def join(kept, arrived):
    rows, depth = kept.shape
    return pl.pallas_call(
        join_kernel,
        out_shape=jax.ShapeDtypeStruct((2 * rows, depth), kept.dtype),
        cost_estimate=pl.CostEstimate(flops=0, bytes_accessed=8 * kept.size, transcendentals=0),
        compiler_params=pltpu.CompilerParams(vmem_limit_bytes=2**20 + 8 * kept.size),
        name="join",
    )(kept, arrived)


def local(n_vocab, n_chip, hidden, unembed, targets):
    heads, tok_rows, depth = hidden.shape
    block = heads * tok_rows
    width = unembed.shape[1]
    n_chips = n_vocab * n_chip
    flows = gather_orders(n_vocab, n_chip)
    rows = n_chips * block

    other_columns = to_other_core(unembed, n_chips)
    cut = depth // 128 * 2 // 3 * 128
    own_rows = hidden.reshape(block, depth)
    kept = [own_rows[:, :cut], own_rows[:, cut:]]
    arrived = [None, None]
    stages = len(flows[0][0])
    for number in range(stages):
        for flow in range(2):
            masks = (flows[flow][0][number], flows[flow][1][number])
            arrived[flow] = exchange(kept[flow], masks, n_chips)
        if number < stages - 1:
            for flow in range(2):
                kept[flow] = join(kept[flow], arrived[flow])
    own_near, other_near = unembed, load(other_columns)
    cost = pl.CostEstimate(
        flops=2 * rows * width * depth, bytes_accessed=(rows + 4 * width) * depth, transcendentals=0
    )
    held = 2 * (rows + 2 * width) * depth + 4 * rows * (8 * width + 3 * rows + 8 * n_chips)
    params = pltpu.CompilerParams(vmem_limit_bytes=held + 2**21)
    logits = jax.ShapeDtypeStruct((rows, 2 * width), jnp.float32)
    partial, wanted = pl.pallas_call(
        functools.partial(kept_kernel, flows, block, n_chips),
        out_shape=(logits, jax.ShapeDtypeStruct((rows, 128), jnp.int32)),
        cost_estimate=cost,
        compiler_params=params,
        name="kept",
    )(targets, kept[0], kept[1], own_near, other_near)
    partial = pl.pallas_call(
        functools.partial(first_kernel, flows, block, n_chips),
        out_shape=logits,
        cost_estimate=cost,
        compiler_params=params,
        name="first",
    )(arrived[0], own_near, other_near, partial)
    stats = pl.pallas_call(
        functools.partial(stats_kernel, flows, block, n_chips),
        out_shape=jax.ShapeDtypeStruct((2, rows), jnp.float32),
        scratch_shapes=[pltpu.VMEM((rows, 2 * width), jnp.float32)],
        cost_estimate=cost,
        compiler_params=params,
        name="stats",
    )(wanted, arrived[1], own_near, other_near, partial)
    small = pltpu.CompilerParams(vmem_limit_bytes=2**20 + 4 * 4 * n_chips * 8 * rows)
    sent = pl.pallas_call(
        pack_kernel,
        out_shape=jax.ShapeDtypeStruct((n_chips, 4, rows), jnp.float32),
        compiler_params=small,
        name="pack",
    )(stats, to_other_core(stats, n_chips))
    received = lax.all_to_all(
        sent, AXIS, split_axis=0, concat_axis=0, tiled=True, axis_index_groups=team_devices(n_chips)
    )
    token_loss, total = pl.pallas_call(
        functools.partial(loss_kernel, n_chips, block, tok_rows),
        out_shape=(jax.ShapeDtypeStruct((heads, tok_rows), jnp.float32), jax.ShapeDtypeStruct((1, 1), jnp.float32)),
        compiler_params=small,
        name="loss",
    )(received)
    return token_loss, total.reshape(())


def solution(mesh):
    n_vocab, n_data = mesh.shape["vocab"], mesh.shape["dp"]
    line = Mesh(mesh.devices.reshape(-1), (AXIS,))
    return jax.shard_map(
        functools.partial(local, n_vocab, n_data // 2),
        mesh=line,
        in_specs=(P(None, AXIS, None), P(None, AXIS), P()),
        out_specs=(P(None, AXIS), P()),
        check_vma=False,
    )
```

time: 69.6 us -> 68.5 us (0.984)
  starting transfers between devices: 16.1 us -> 17.9 us
  waiting for transfers between devices: 29.9 us -> 28.7 us
  blocking collectives: 15 us -> 13.9 us
    ppermute x10, starting transfers between devices: 16.1 us -> 17.9 us  [the longest x8 15.7 us: exchange(): return lax.ppermute(value, AXIS, sorted(pairs))]
    all_to_all x1, blocking collectives: 15 us -> 13.9 us  [local(): lax.all_to_all(sent, AXIS, split_axis=0, concat_axis=0, tiled=True, axis_...]
    ppermute x10, waiting for transfers between devices: 29.9 us -> 28.7 us  [the longest x8 27.9 us: exchange(): return lax.ppermute(value, AXIS, sorted(pairs))]
    pallas_call x4 -> x5, Pallas kernels: 3.95 us -> 3.97 us  [the longest x1 1.44 us: local(): pl.pallas_call(functools.partial(kept_kernel, flows, block, n_chips), out...]
where the time goes in v5:
time: 68.5 us; the launch traced here: 68.3 us
  waiting for transfers between devices  28.7 us (42%)
  starting transfers between devices  17.9 us (26%)
  blocking collectives  13.9 us (20%)
  Pallas kernels  6.13 us (9%)
  local copies, waits for them, and re-layouts  0.95 us (1%)
  between operations  0.73 us (1%)
    ppermute x8, waiting for transfers between devices, exchange(): return lax.ppermute(value, AXIS, sorted(pairs))  27.9 us
    ppermute x8, starting transfers between devices, exchange(): return lax.ppermute(value, AXIS, sorted(pairs))  15.7 us
    all_to_all x1, blocking collectives, local(): lax.all_to_all(sent, AXIS, split_axis=0, concat_axis=0, tiled=True, axis_...  13.9 us
    ppermute x2, starting transfers between devices, to_other_core(): return lax.ppermute(value, AXIS, pairs)  2.18 us
    pallas_call x1, Pallas kernels, load(): pl.pallas_call(load_kernel, out_shape=jax.ShapeDtypeStruct(columns.shape,...  2.05 us
    pallas_call x1, Pallas kernels, local(): pl.pallas_call(functools.partial(kept_kernel, flows, block, n_chips), out...  1.44 us
  transfers between devices with their start and end apart: 10, of which 8 were waited for; matrix products, arithmetic and copies ran while one was open for 1% of the time, Pallas kernels for 7%

profile of v5, /device:TPU:0, one launch (start us, length us, event | category | flops | bytes accessed | tf_op | source)
XLA Modules:
  0.0 68.3 jit_solution(11626705589967841187)
XLA Ops:
  0.6 0.6 collective-permute-start.6
  1.2 0.9 %reshape.10 = bf16[8,7168]{1,0:T(8,128)(2,1)S(1)} reshape(bf16[2,4,7168]{2,1,0:T(4,128)(2,1)} %param.3) | data formatting | bytes 229376 | tf_op jit(solution)/shard_map/reshape | solution.py:184
  2.1 3.8 %collective-permute-start = (bf16[8,4736]{1,0:T(8,128)(2,1)S(1)}, bf16[8,4736]{1,0:T(8,128)(2,1)S(1)}, u32[]{:S(2)}, u32[]{:S(2)}) collective-permute-start(bf16[8,4736]{1,0:T(8,128)(2,1)S(1)} %slice.8.kept), channel_id=1, source_target_pairs={{0,17},{1,8},{2,11},{3,18},{4,13},{5,20},{6,23},{7,14},{8,1},{9,24... | collective-permute-start | bytes 227336 | tf_op jit(solution)/shard_map/ppermute | solution.py:46
  5.9 2.1 %collective-permute-done.arrived = bf16[8,4736]{1,0:T(8,128)(2,1)S(1)} collective-permute-done((bf16[8,4736]{1,0:T(8,128)(2,1)S(1)}, bf16[8,4736]{1,0:T(8,128)(2,1)S(1)}, u32[]{:S(2)}, u32[]{:S(2)}) %collective-permute-start) | collective-permute-done | bytes 75808 | tf_op jit(solution)/shard_map/ppermute | solution.py:46
  8.0 1.9 %collective-permute-start.1 = (bf16[16,4736]{1,0:T(8,128)(2,1)S(1)}, bf16[16,4736]{1,0:T(8,128)(2,1)S(1)}, u32[]{:S(2)}, u32[]{:S(2)}) collective-permute-start(bf16[16,4736]{1,0:T(8,128)(2,1)S(1)} %join.6.kept), channel_id=1, source_target_pairs={{0,9},{1,16},{2,19},{3,10},{4,21},{5,12},{6,15},{7,22},{8,25},{9,0... | collective-permute-start | bytes 454664 | tf_op jit(solution)/shard_map/ppermute | solution.py:46
  9.9 4.3 %collective-permute-done.1.arrived = bf16[16,4736]{1,0:T(8,128)(2,1)S(1)} collective-permute-done((bf16[16,4736]{1,0:T(8,128)(2,1)S(1)}, bf16[16,4736]{1,0:T(8,128)(2,1)S(1)}, u32[]{:S(2)}, u32[]{:S(2)}) %collective-permute-start.1) | collective-permute-done | bytes 151584 | tf_op jit(solution)/shard_map/ppermute | solution.py:46
  14.2 1.5 %collective-permute-start.2 = (bf16[32,4736]{1,0:T(8,128)(2,1)S(1)}, bf16[32,4736]{1,0:T(8,128)(2,1)S(1)}, u32[]{:S(2)}, u32[]{:S(2)}) collective-permute-start(bf16[32,4736]{1,0:T(8,128)(2,1)S(1)} %join.7.kept), channel_id=1, source_target_pairs={{0,5},{1,2},{2,1},{3,6},{4,7},{5,0},{6,3},{7,4},{8,11},{9,12},{10,... | collective-permute-start | bytes 909320 | tf_op jit(solution)/shard_map/ppermute | solution.py:46
  15.7 4.8 %collective-permute-done.2.arrived = bf16[32,4736]{1,0:T(8,128)(2,1)S(1)} collective-permute-done((bf16[32,4736]{1,0:T(8,128)(2,1)S(1)}, bf16[32,4736]{1,0:T(8,128)(2,1)S(1)}, u32[]{:S(2)}, u32[]{:S(2)}) %collective-permute-start.2) | collective-permute-done | bytes 303136 | tf_op jit(solution)/shard_map/ppermute | solution.py:46
  20.6 1.4 %collective-permute-start.8 = (bf16[64,4736]{1,0:T(8,128)(2,1)S(1)}, bf16[64,4736]{1,0:T(8,128)(2,1)S(1)}, u32[]{:S(2)}, u32[]{:S(2)}) collective-permute-start(bf16[64,4736]{1,0:T(8,128)(2,1)S(1)} %join.8.kept_a), channel_id=1, source_target_pairs={{0,3},{1,4},{2,7},{3,0},{4,1},{5,6},{6,5},{7,2},{8,13},{9,10},{10,... | collective-permute-start | bytes 1818632 | tf_op jit(solution)/shard_map/ppermute | solution.py:46
  22.0 0.4 collective-permute-start.3
  22.4 8.2 %collective-permute-done.3.arrived = bf16[8,2432]{1,0:T(8,128)(2,1)S(1)} collective-permute-done((bf16[8,2432]{1,0:T(8,128)(2,1)S(1)}, bf16[8,2432]{1,0:T(8,128)(2,1)S(1)}, u32[]{:S(2)}, u32[]{:S(2)}) %collective-permute-start.3) | collective-permute-done | bytes 38944 | tf_op jit(solution)/shard_map/ppermute | solution.py:46
  30.5 1.9 %collective-permute-start.4 = (bf16[16,2432]{1,0:T(8,128)(2,1)S(1)}, bf16[16,2432]{1,0:T(8,128)(2,1)S(1)}, u32[]{:S(2)}, u32[]{:S(2)}) collective-permute-start(bf16[16,2432]{1,0:T(8,128)(2,1)S(1)} %join.9.kept), channel_id=1, source_target_pairs={{0,5},{1,2},{2,1},{3,6},{4,7},{5,0},{6,3},{7,4},{8,11},{9,12},{10,... | collective-permute-start | bytes 233480 | tf_op jit(solution)/shard_map/ppermute | solution.py:46
  32.5 2.1 %collective-permute-done.4.arrived = bf16[16,2432]{1,0:T(8,128)(2,1)S(1)} collective-permute-done((bf16[16,2432]{1,0:T(8,128)(2,1)S(1)}, bf16[16,2432]{1,0:T(8,128)(2,1)S(1)}, u32[]{:S(2)}, u32[]{:S(2)}) %collective-permute-start.4) | collective-permute-done | bytes 77856 | tf_op jit(solution)/shard_map/ppermute | solution.py:46
  34.6 2.3 %collective-permute-start.5 = (bf16[32,2432]{1,0:T(8,128)(2,1)S(1)}, bf16[32,2432]{1,0:T(8,128)(2,1)S(1)}, u32[]{:S(2)}, u32[]{:S(2)}) collective-permute-start(bf16[32,2432]{1,0:T(8,128)(2,1)S(1)} %join.10.kept), channel_id=1, source_target_pairs={{0,17},{1,8},{2,11},{3,18},{4,13},{5,20},{6,23},{7,14},{8,1},{9,24... | collective-permute-start | bytes 466952 | tf_op jit(solution)/shard_map/ppermute | solution.py:46
  36.9 3.6 %collective-permute-done.5.arrived = bf16[32,2432]{1,0:T(8,128)(2,1)S(1)} collective-permute-done((bf16[32,2432]{1,0:T(8,128)(2,1)S(1)}, bf16[32,2432]{1,0:T(8,128)(2,1)S(1)}, u32[]{:S(2)}, u32[]{:S(2)}) %collective-permute-start.5) | collective-permute-done | bytes 155680 | tf_op jit(solution)/shard_map/ppermute | solution.py:46
  40.5 0.0 copy-start
  40.5 0.0 copy-start.1
  40.6 2.5 %collective-permute-start.7 = (bf16[64,2432]{1,0:T(8,128)(2,1)S(1)}, bf16[64,2432]{1,0:T(8,128)(2,1)S(1)}, u32[]{:S(2)}, u32[]{:S(2)}) collective-permute-start(bf16[64,2432]{1,0:T(8,128)(2,1)S(1)} %join.11.kept_b), channel_id=1, source_target_pairs={{0,9},{1,16},{2,19},{3,10},{4,21},{5,12},{6,15},{7,22},{8,25},{9,0... | collective-permute-start | bytes 933896 | tf_op jit(solution)/shard_map/ppermute | solution.py:46
  43.0 0.0 collective-permute-done.6.source
  43.0 2.0 %shard_map.50.other = bf16[7168,256]{1,0:T(8,128)(2,1)S(1)} custom-call(bf16[7168,256]{1,0:T(8,128)(2,1)} %collective-permute-done.6.source), custom_call_target="tpu_custom_call" | custom-call | bytes 7340032 | tf_op jit(solution)/shard_map/pallas_call | solution.py:152
  45.1 0.0 copy-done
  45.1 0.0 copy-done.1
  45.1 1.4 %kept.1 = (f32[128,512]{1,0:T(8,128)S(1)}, s32[128,128]{1,0:T(8,128)S(1)}) custom-call(s32[2,128]{1,0:T(2,128)S(1)} %copy-done.1, bf16[64,4736]{1,0:T(8,128)(2,1)S(1)} %join.8.kept_a, bf16[64,2432]{1,0:T(8,128)(2,1)S(1)} %join.11.kept_b, bf16[7168,256]{1,0:T(8,128)(2,1)S(1)} %copy-done, bf16[7168,256]{1,0:T(8,128)(2,1)S(1)} %shard_map.50.other), custom_call_target="tpu_custom_call" | custom-call | flops 469762048 | bytes 8257536 | tf_op jit(solution)/shard_map/kept/pallas_call | solution.py:202
  46.6 0.0 collective-permute-done.8.arrived
  46.6 1.0 %first.1.partial = f32[128,512]{1,0:T(8,128)S(1)} custom-call(bf16[64,4736]{1,0:T(8,128)(2,1)S(1)} %collective-permute-done.8.arrived, bf16[7168,256]{1,0:T(8,128)(2,1)S(1)} %copy-done, bf16[7168,256]{1,0:T(8,128)(2,1)S(1)} %shard_map.50.other, f32[128,512]{1,0:T(8,128)S(1)} %get-tuple-element.7.partial), custom_call_target="tpu_custom_call" | custom-call | flops 469762048 | bytes 8257536 | tf_op jit(solution)/shard_map/first/pallas_call | solution.py:209
  47.6 2.9 %collective-permute-done.7.arrived = bf16[64,2432]{1,0:T(8,128)(2,1)S(1)} collective-permute-done((bf16[64,2432]{1,0:T(8,128)(2,1)S(1)}, bf16[64,2432]{1,0:T(8,128)(2,1)S(1)}, u32[]{:S(2)}, u32[]{:S(2)}) %collective-permute-start.7) | collective-permute-done | bytes 311328 | tf_op jit(solution)/shard_map/ppermute | solution.py:46
  50.4 0.8 %stats.1.own = f32[2,128]{1,0:T(2,128)S(1)} custom-call(s32[128,128]{1,0:T(8,128)S(1)} %get-tuple-element.6.wanted, bf16[64,2432]{1,0:T(8,128)(2,1)S(1)} %collective-permute-done.7.arrived, bf16[7168,256]{1,0:T(8,128)(2,1)S(1)} %copy-done, bf16[7168,256]{1,0:T(8,128)(2,1)S(1)} %shard_map.50.other, f32[128,512]{1,0:T(8,128)S(1)} %first.1.partial), custom_call_target="tpu_custom_call" | custom-call | flops 469762048 | bytes 8257536 | tf_op jit(solution)/shard_map/stats/pallas_call | solution.py:216
  51.3 1.6 %collective-permute-start.9 = (f32[2,128]{1,0:T(2,128)S(1)}, f32[2,128]{1,0:T(2,128)S(1)}, u32[]{:S(2)}, u32[]{:S(2)}) collective-permute-start(f32[2,128]{1,0:T(2,128)S(1)} %stats.1.own), channel_id=1, source_target_pairs={{0,1},{1,0},{2,3},{3,2},{4,5},{5,4},{6,7},{7,6},{8,9},{9,8},{10,11... | collective-permute-start | bytes 3080 | tf_op jit(solution)/shard_map/ppermute | solution.py:51
  52.9 0.8 %collective-permute-done.9.other = f32[2,128]{1,0:T(2,128)S(1)} collective-permute-done((f32[2,128]{1,0:T(2,128)S(1)}, f32[2,128]{1,0:T(2,128)S(1)}, u32[]{:S(2)}, u32[]{:S(2)}) %collective-permute-start.9) | collective-permute-done | bytes 1056 | tf_op jit(solution)/shard_map/ppermute | solution.py:51
  53.7 13.9 %all_to_all.5.received = f32[16,4,128]{2,1,0:T(4,128)S(1)} all-to-all(f32[16,4,128]{2,1,0:T(4,128)S(1)} %pack.1), channel_id=1, replica_groups={{0,3,5,6,9,10,12,15,17,18,20,23,24,27,29,30},{1,2,4,7,8,11,13,14,16,19,..., dimensions={0} | all-to-all | bytes 65536 | tf_op jit(solution)/shard_map/all_to_all | solution.py:231
  67.6 0.7 %loss.1 = (f32[2,4]{1,0:T(2,128)}, f32[1,1]{1,0:T(1,128)}) custom-call(f32[16,4,128]{2,1,0:T(4,128)S(1)} %all_to_all.5.received), custom_call_target="tpu_custom_call" | custom-call | tf_op jit(solution)/shard_map/loss/pallas_call | solution.py:234
  (9 shorter events, 0.1 us)
Async XLA Ops:
  0.6 42.4 %collective-permute-start.6 = (bf16[7168,256]{1,0:T(8,128)(2,1)}, bf16[7168,256]{1,0:T(8,128)(2,1)}, u32[]{:S(2)}, u32[]{:S(2)}) collective-permute-start(bf16[7168,256]{1,0:T(8,128)(2,1)} %own.5), channel_id=1, source_target_pairs={{0,1},{1,0},{2,3},{3,2},{4,5},{5,4},{6,7},{7,6},{8,9},{9,8},{10,11... | collective-permute-start | bytes 11010056 | tf_op jit(solution)/shard_map/ppermute | solution.py:51
  2.1 5.8 %collective-permute-start = (bf16[8,4736]{1,0:T(8,128)(2,1)S(1)}, bf16[8,4736]{1,0:T(8,128)(2,1)S(1)}, u32[]{:S(2)}, u32[]{:S(2)}) collective-permute-start(bf16[8,4736]{1,0:T(8,128)(2,1)S(1)} %slice.8.kept), channel_id=1, source_target_pairs={{0,17},{1,8},{2,11},{3,18},{4,13},{5,20},{6,23},{7,14},{8,1},{9,24... | collective-permute-start | bytes 227336 | tf_op jit(solution)/shard_map/ppermute | solution.py:46
  8.0 6.2 %collective-permute-start.1 = (bf16[16,4736]{1,0:T(8,128)(2,1)S(1)}, bf16[16,4736]{1,0:T(8,128)(2,1)S(1)}, u32[]{:S(2)}, u32[]{:S(2)}) collective-permute-start(bf16[16,4736]{1,0:T(8,128)(2,1)S(1)} %join.6.kept), channel_id=1, source_target_pairs={{0,9},{1,16},{2,19},{3,10},{4,21},{5,12},{6,15},{7,22},{8,25},{9,0... | collective-permute-start | bytes 454664 | tf_op jit(solution)/shard_map/ppermute | solution.py:46
  14.2 6.3 %collective-permute-start.2 = (bf16[32,4736]{1,0:T(8,128)(2,1)S(1)}, bf16[32,4736]{1,0:T(8,128)(2,1)S(1)}, u32[]{:S(2)}, u32[]{:S(2)}) collective-permute-start(bf16[32,4736]{1,0:T(8,128)(2,1)S(1)} %join.7.kept), channel_id=1, source_target_pairs={{0,5},{1,2},{2,1},{3,6},{4,7},{5,0},{6,3},{7,4},{8,11},{9,12},{10,... | collective-permute-start | bytes 909320 | tf_op jit(solution)/shard_map/ppermute | solution.py:46
  20.6 26.0 %collective-permute-start.8 = (bf16[64,4736]{1,0:T(8,128)(2,1)S(1)}, bf16[64,4736]{1,0:T(8,128)(2,1)S(1)}, u32[]{:S(2)}, u32[]{:S(2)}) collective-permute-start(bf16[64,4736]{1,0:T(8,128)(2,1)S(1)} %join.8.kept_a), channel_id=1, source_target_pairs={{0,3},{1,4},{2,7},{3,0},{4,1},{5,6},{6,5},{7,2},{8,13},{9,10},{10,... | collective-permute-start | bytes 1818632 | tf_op jit(solution)/shard_map/ppermute | solution.py:46
  22.0 8.5 %collective-permute-start.3 = (bf16[8,2432]{1,0:T(8,128)(2,1)S(1)}, bf16[8,2432]{1,0:T(8,128)(2,1)S(1)}, u32[]{:S(2)}, u32[]{:S(2)}) collective-permute-start(bf16[8,2432]{1,0:T(8,128)(2,1)S(1)} %slice.9.kept), channel_id=1, source_target_pairs={{0,3},{1,4},{2,7},{3,0},{4,1},{5,6},{6,5},{7,2},{8,13},{9,10},{10,... | collective-permute-start | bytes 116744 | tf_op jit(solution)/shard_map/ppermute | solution.py:46
  30.5 4.0 %collective-permute-start.4 = (bf16[16,2432]{1,0:T(8,128)(2,1)S(1)}, bf16[16,2432]{1,0:T(8,128)(2,1)S(1)}, u32[]{:S(2)}, u32[]{:S(2)}) collective-permute-start(bf16[16,2432]{1,0:T(8,128)(2,1)S(1)} %join.9.kept), channel_id=1, source_target_pairs={{0,5},{1,2},{2,1},{3,6},{4,7},{5,0},{6,3},{7,4},{8,11},{9,12},{10,... | collective-permute-start | bytes 233480 | tf_op jit(solution)/shard_map/ppermute | solution.py:46
  34.6 5.9 %collective-permute-start.5 = (bf16[32,2432]{1,0:T(8,128)(2,1)S(1)}, bf16[32,2432]{1,0:T(8,128)(2,1)S(1)}, u32[]{:S(2)}, u32[]{:S(2)}) collective-permute-start(bf16[32,2432]{1,0:T(8,128)(2,1)S(1)} %join.10.kept), channel_id=1, source_target_pairs={{0,17},{1,8},{2,11},{3,18},{4,13},{5,20},{6,23},{7,14},{8,1},{9,24... | collective-permute-start | bytes 466952 | tf_op jit(solution)/shard_map/ppermute | solution.py:46
  40.5 4.6 %copy-start = (bf16[7168,256]{1,0:T(8,128)(2,1)S(1)}, bf16[7168,256]{1,0:T(8,128)(2,1)}, u32[]{:S(2)}) copy-start(bf16[7168,256]{1,0:T(8,128)(2,1)} %own.5) | copy-start | bytes 11010052
  40.5 4.6 %copy-start.1 = (s32[2,128]{1,0:T(2,128)S(1)}, s32[2,128]{1,0:T(2,128)}, u32[]{:S(2)}) copy-start(s32[2,128]{1,0:T(2,128)} %targets.1) | copy-start | bytes 3076
  40.6 9.9 %collective-permute-start.7 = (bf16[64,2432]{1,0:T(8,128)(2,1)S(1)}, bf16[64,2432]{1,0:T(8,128)(2,1)S(1)}, u32[]{:S(2)}, u32[]{:S(2)}) collective-permute-start(bf16[64,2432]{1,0:T(8,128)(2,1)S(1)} %join.11.kept_b), channel_id=1, source_target_pairs={{0,9},{1,16},{2,19},{3,10},{4,21},{5,12},{6,15},{7,22},{8,25},{9,0... | collective-permute-start | bytes 933896 | tf_op jit(solution)/shard_map/ppermute | solution.py:46
  51.3 2.4 %collective-permute-start.9 = (f32[2,128]{1,0:T(2,128)S(1)}, f32[2,128]{1,0:T(2,128)S(1)}, u32[]{:S(2)}, u32[]{:S(2)}) collective-permute-start(f32[2,128]{1,0:T(2,128)S(1)} %stats.1.own), channel_id=1, source_target_pairs={{0,1},{1,0},{2,3},{3,2},{4,5},{5,4},{6,7},{7,6},{8,9},{9,8},{10,11... | collective-permute-start | bytes 3080 | tf_op jit(solution)/shard_map/ppermute | solution.py:51

commit v6 on v5

--- a/solution.py
+++ b/solution.py
@@ -19,7 +19,7 @@
     far = [n_chip * mask for mask in bits(n_vocab)[1:]]
     return (
         (far[::-1] + near[::-1], far + near),
-        (near + far[::-1], near[::-1] + far),
+        (near + far, near[::-1] + far[::-1]),
     )
 
 
@@ -77,6 +77,13 @@
     copy = pltpu.make_async_copy(source, target, arrival)
     copy.start()
     copy.wait()
+
+
+def split_kernel(hidden, out_a, out_b):
+    rows = jnp.concatenate([hidden[head] for head in range(hidden.shape[0])], axis=0)
+    cut = out_a.shape[1]
+    out_a[...] = rows[:, :cut]
+    out_b[...] = rows[:, cut:]
 
 
 def join_kernel(kept, arrived, out):
@@ -181,8 +188,14 @@
 
     other_columns = to_other_core(unembed, n_chips)
     cut = depth // 128 * 2 // 3 * 128
-    own_rows = hidden.reshape(block, depth)
-    kept = [own_rows[:, :cut], own_rows[:, cut:]]
+    kept = list(
+        pl.pallas_call(
+            split_kernel,
+            out_shape=tuple(jax.ShapeDtypeStruct((block, count), hidden.dtype) for count in (cut, depth - cut)),
+            compiler_params=pltpu.CompilerParams(vmem_limit_bytes=2**20 + 8 * hidden.size),
+            name="split",
+        )(hidden)
+    )
     arrived = [None, None]
     stages = len(flows[0][0])
     for number in range(stages):

time: 68.5 us -> 67.1 us (0.980)
  waiting for transfers between devices: 28.7 us -> 30.5 us
  Pallas kernels: 6.13 us -> 4.38 us
  starting transfers between devices: 17.9 us -> 16.9 us
    ppermute x8, waiting for transfers between devices: 27.9 us -> 29.7 us  [exchange(): return lax.ppermute(value, AXIS, sorted(pairs))]
    pallas_call x1, Pallas kernels: 2.05 us -> 0.26 us  [load(): pl.pallas_call(load_kernel, out_shape=jax.ShapeDtypeStruct(columns.shape,...]
    ppermute x2, starting transfers between devices: 2.18 us -> 1.15 us  [to_other_core(): return lax.ppermute(value, AXIS, pairs)]
    reshape x1 -> x0, local copies, waits for them, and re-layouts: 0.93 us -> none  [local(): own_rows = hidden.reshape(block, depth)]
    unnamed x4 -> x6, local copies, waits for them, and re-layouts: 0.01 us -> 0.91 us
  transfers between devices with their start and end apart: 10 -> 10, of which waited for: 8 -> 8; matrix products, arithmetic and copies ran while one was open for 1% -> 0% of each run, Pallas kernels for 7% -> 4%
where the time goes in v6:
time: 67.1 us; the launch traced here: 66.9 us
  waiting for transfers between devices  30.5 us (45%)
  starting transfers between devices  16.9 us (25%)
  blocking collectives  13.5 us (20%)
  Pallas kernels  4.38 us (7%)
  local copies, waits for them, and re-layouts  0.91 us (1%)
  between operations  0.73 us (1%)
    ppermute x8, waiting for transfers between devices, exchange(): return lax.ppermute(value, AXIS, sorted(pairs))  29.7 us
    ppermute x8, starting transfers between devices, exchange(): return lax.ppermute(value, AXIS, sorted(pairs))  15.8 us
    all_to_all x1, blocking collectives, local(): lax.all_to_all(sent, AXIS, split_axis=0, concat_axis=0, tiled=True, axis_...  13.5 us
    pallas_call x1, Pallas kernels, local(): pl.pallas_call(functools.partial(kept_kernel, flows, block, n_chips), out...  1.45 us
  transfers between devices with their start and end apart: 10, of which 8 were waited for; matrix products, arithmetic and copies ran while one was open for 0% of the time, Pallas kernels for 4%

profile of v6, /device:TPU:0, one launch (start us, length us, event | category | flops | bytes accessed | tf_op | source)
XLA Modules:
  0.0 66.9 jit_solution(2938119516446666364)
XLA Ops:
  0.6 0.6 collective-permute-start.6
  1.2 0.0 copy-start.1
  1.2 0.9 %copy-done.1 = bf16[2,4,7168]{2,1,0:T(4,128)(2,1)S(1)} copy-done((bf16[2,4,7168]{2,1,0:T(4,128)(2,1)S(1)}, bf16[2,4,7168]{2,1,0:T(4,128)(2,1)}, u32[]{:S(2)}) %copy-start.1) | copy-done | bytes 114712
  2.1 3.8 %collective-permute-start = (bf16[8,4736]{1,0:T(8,128)(2,1)S(1)}, bf16[8,4736]{1,0:T(8,128)(2,1)S(1)}, u32[]{:S(2)}, u32[]{:S(2)}) collective-permute-start(bf16[8,4736]{1,0:T(8,128)(2,1)S(1)} %get-tuple-element.8.kept), channel_id=1, source_target_pairs={{0,17},{1,8},{2,11},{3,18},{4,13},{5,20},{6,23},{7,14},{8,1},{9,24... | collective-permute-start | bytes 227336 | tf_op jit(solution)/shard_map/ppermute | solution.py:46
  5.9 2.1 %collective-permute-done.arrived = bf16[8,4736]{1,0:T(8,128)(2,1)S(1)} collective-permute-done((bf16[8,4736]{1,0:T(8,128)(2,1)S(1)}, bf16[8,4736]{1,0:T(8,128)(2,1)S(1)}, u32[]{:S(2)}, u32[]{:S(2)}) %collective-permute-start) | collective-permute-done | bytes 75808 | tf_op jit(solution)/shard_map/ppermute | solution.py:46
  8.0 1.9 %collective-permute-start.1 = (bf16[16,4736]{1,0:T(8,128)(2,1)S(1)}, bf16[16,4736]{1,0:T(8,128)(2,1)S(1)}, u32[]{:S(2)}, u32[]{:S(2)}) collective-permute-start(bf16[16,4736]{1,0:T(8,128)(2,1)S(1)} %join.6.kept), channel_id=1, source_target_pairs={{0,9},{1,16},{2,19},{3,10},{4,21},{5,12},{6,15},{7,22},{8,25},{9,0... | collective-permute-start | bytes 454664 | tf_op jit(solution)/shard_map/ppermute | solution.py:46
  9.9 4.3 %collective-permute-done.1.arrived = bf16[16,4736]{1,0:T(8,128)(2,1)S(1)} collective-permute-done((bf16[16,4736]{1,0:T(8,128)(2,1)S(1)}, bf16[16,4736]{1,0:T(8,128)(2,1)S(1)}, u32[]{:S(2)}, u32[]{:S(2)}) %collective-permute-start.1) | collective-permute-done | bytes 151584 | tf_op jit(solution)/shard_map/ppermute | solution.py:46
  14.2 1.5 %collective-permute-start.2 = (bf16[32,4736]{1,0:T(8,128)(2,1)S(1)}, bf16[32,4736]{1,0:T(8,128)(2,1)S(1)}, u32[]{:S(2)}, u32[]{:S(2)}) collective-permute-start(bf16[32,4736]{1,0:T(8,128)(2,1)S(1)} %join.7.kept), channel_id=1, source_target_pairs={{0,5},{1,2},{2,1},{3,6},{4,7},{5,0},{6,3},{7,4},{8,11},{9,12},{10,... | collective-permute-start | bytes 909320 | tf_op jit(solution)/shard_map/ppermute | solution.py:46
  15.7 4.8 %collective-permute-done.2.arrived = bf16[32,4736]{1,0:T(8,128)(2,1)S(1)} collective-permute-done((bf16[32,4736]{1,0:T(8,128)(2,1)S(1)}, bf16[32,4736]{1,0:T(8,128)(2,1)S(1)}, u32[]{:S(2)}, u32[]{:S(2)}) %collective-permute-start.2) | collective-permute-done | bytes 303136 | tf_op jit(solution)/shard_map/ppermute | solution.py:46
  20.5 1.4 %collective-permute-start.8 = (bf16[64,4736]{1,0:T(8,128)(2,1)S(1)}, bf16[64,4736]{1,0:T(8,128)(2,1)S(1)}, u32[]{:S(2)}, u32[]{:S(2)}) collective-permute-start(bf16[64,4736]{1,0:T(8,128)(2,1)S(1)} %join.8.kept_a), channel_id=1, source_target_pairs={{0,3},{1,4},{2,7},{3,0},{4,1},{5,6},{6,5},{7,2},{8,13},{9,10},{10,... | collective-permute-start | bytes 1818632 | tf_op jit(solution)/shard_map/ppermute | solution.py:46
  22.0 0.4 collective-permute-start.3
  22.4 8.2 %collective-permute-done.3.arrived = bf16[8,2432]{1,0:T(8,128)(2,1)S(1)} collective-permute-done((bf16[8,2432]{1,0:T(8,128)(2,1)S(1)}, bf16[8,2432]{1,0:T(8,128)(2,1)S(1)}, u32[]{:S(2)}, u32[]{:S(2)}) %collective-permute-start.3) | collective-permute-done | bytes 38944 | tf_op jit(solution)/shard_map/ppermute | solution.py:46
  30.5 1.9 %collective-permute-start.4 = (bf16[16,2432]{1,0:T(8,128)(2,1)S(1)}, bf16[16,2432]{1,0:T(8,128)(2,1)S(1)}, u32[]{:S(2)}, u32[]{:S(2)}) collective-permute-start(bf16[16,2432]{1,0:T(8,128)(2,1)S(1)} %join.9.kept), channel_id=1, source_target_pairs={{0,5},{1,2},{2,1},{3,6},{4,7},{5,0},{6,3},{7,4},{8,11},{9,12},{10,... | collective-permute-start | bytes 233480 | tf_op jit(solution)/shard_map/ppermute | solution.py:46
  32.5 2.1 %collective-permute-done.4.arrived = bf16[16,2432]{1,0:T(8,128)(2,1)S(1)} collective-permute-done((bf16[16,2432]{1,0:T(8,128)(2,1)S(1)}, bf16[16,2432]{1,0:T(8,128)(2,1)S(1)}, u32[]{:S(2)}, u32[]{:S(2)}) %collective-permute-start.4) | collective-permute-done | bytes 77856 | tf_op jit(solution)/shard_map/ppermute | solution.py:46
  34.5 1.5 %collective-permute-start.5 = (bf16[32,2432]{1,0:T(8,128)(2,1)S(1)}, bf16[32,2432]{1,0:T(8,128)(2,1)S(1)}, u32[]{:S(2)}, u32[]{:S(2)}) collective-permute-start(bf16[32,2432]{1,0:T(8,128)(2,1)S(1)} %join.10.kept), channel_id=1, source_target_pairs={{0,9},{1,16},{2,19},{3,10},{4,21},{5,12},{6,15},{7,22},{8,25},{9,0... | collective-permute-start | bytes 466952 | tf_op jit(solution)/shard_map/ppermute | solution.py:46
  36.0 3.9 %collective-permute-done.5.arrived = bf16[32,2432]{1,0:T(8,128)(2,1)S(1)} collective-permute-done((bf16[32,2432]{1,0:T(8,128)(2,1)S(1)}, bf16[32,2432]{1,0:T(8,128)(2,1)S(1)}, u32[]{:S(2)}, u32[]{:S(2)}) %collective-permute-start.5) | collective-permute-done | bytes 155680 | tf_op jit(solution)/shard_map/ppermute | solution.py:46
  39.9 0.0 copy-start
  39.9 0.0 copy-start.2
  39.9 3.4 %collective-permute-start.7 = (bf16[64,2432]{1,0:T(8,128)(2,1)S(1)}, bf16[64,2432]{1,0:T(8,128)(2,1)S(1)}, u32[]{:S(2)}, u32[]{:S(2)}) collective-permute-start(bf16[64,2432]{1,0:T(8,128)(2,1)S(1)} %join.11.kept_b), channel_id=1, source_target_pairs={{0,17},{1,8},{2,11},{3,18},{4,13},{5,20},{6,23},{7,14},{8,1},{9,24... | collective-permute-start | bytes 933896 | tf_op jit(solution)/shard_map/ppermute | solution.py:46
  43.3 0.0 collective-permute-done.6.source
  43.3 0.3 shard_map.50.other
  43.6 0.0 copy-done
  43.6 0.0 copy-done.2
  43.6 1.4 %kept.1 = (f32[128,512]{1,0:T(8,128)S(1)}, s32[128,128]{1,0:T(8,128)S(1)}) custom-call(s32[2,128]{1,0:T(2,128)S(1)} %copy-done.2, bf16[64,4736]{1,0:T(8,128)(2,1)S(1)} %join.8.kept_a, bf16[64,2432]{1,0:T(8,128)(2,1)S(1)} %join.11.kept_b, bf16[7168,256]{1,0:T(8,128)(2,1)S(1)} %copy-done, bf16[7168,256]{1,0:T(8,128)(2,1)S(1)} %shard_map.50.other), custom_call_target="tpu_custom_call" | custom-call | flops 469762048 | bytes 8257536 | tf_op jit(solution)/shard_map/kept/pallas_call | solution.py:215
  45.1 0.0 collective-permute-done.8.arrived
  45.1 1.0 %first.1.partial = f32[128,512]{1,0:T(8,128)S(1)} custom-call(bf16[64,4736]{1,0:T(8,128)(2,1)S(1)} %collective-permute-done.8.arrived, bf16[7168,256]{1,0:T(8,128)(2,1)S(1)} %copy-done, bf16[7168,256]{1,0:T(8,128)(2,1)S(1)} %shard_map.50.other, f32[128,512]{1,0:T(8,128)S(1)} %get-tuple-element.11.partial), custom_call_target="tpu_custom_call" | custom-call | flops 469762048 | bytes 8257536 | tf_op jit(solution)/shard_map/first/pallas_call | solution.py:222
  46.1 4.4 %collective-permute-done.7.arrived = bf16[64,2432]{1,0:T(8,128)(2,1)S(1)} collective-permute-done((bf16[64,2432]{1,0:T(8,128)(2,1)S(1)}, bf16[64,2432]{1,0:T(8,128)(2,1)S(1)}, u32[]{:S(2)}, u32[]{:S(2)}) %collective-permute-start.7) | collective-permute-done | bytes 311328 | tf_op jit(solution)/shard_map/ppermute | solution.py:46
  50.5 0.8 %stats.1.own = f32[2,128]{1,0:T(2,128)S(1)} custom-call(s32[128,128]{1,0:T(8,128)S(1)} %get-tuple-element.10.wanted, bf16[64,2432]{1,0:T(8,128)(2,1)S(1)} %collective-permute-done.7.arrived, bf16[7168,256]{1,0:T(8,128)(2,1)S(1)} %copy-done, bf16[7168,256]{1,0:T(8,128)(2,1)S(1)} %shard_map.50.other, f32[128,512]{1,0:T(8,128)S(1)} %first.1.partial), custom_call_target="tpu_custom_call" | custom-call | flops 469762048 | bytes 8257536 | tf_op jit(solution)/shard_map/stats/pallas_call | solution.py:229
  51.3 0.6 collective-permute-start.9
  51.9 0.8 %collective-permute-done.9.other = f32[2,128]{1,0:T(2,128)S(1)} collective-permute-done((f32[2,128]{1,0:T(2,128)S(1)}, f32[2,128]{1,0:T(2,128)S(1)}, u32[]{:S(2)}, u32[]{:S(2)}) %collective-permute-start.9) | collective-permute-done | bytes 1056 | tf_op jit(solution)/shard_map/ppermute | solution.py:51
  52.8 13.5 %all_to_all.5.received = f32[16,4,128]{2,1,0:T(4,128)S(1)} all-to-all(f32[16,4,128]{2,1,0:T(4,128)S(1)} %pack.1), channel_id=1, replica_groups={{0,3,5,6,9,10,12,15,17,18,20,23,24,27,29,30},{1,2,4,7,8,11,13,14,16,19,..., dimensions={0} | all-to-all | bytes 65536 | tf_op jit(solution)/shard_map/all_to_all | solution.py:244
  66.2 0.7 %loss.1 = (f32[2,4]{1,0:T(2,128)}, f32[1,1]{1,0:T(1,128)}) custom-call(f32[16,4,128]{2,1,0:T(4,128)S(1)} %all_to_all.5.received), custom_call_target="tpu_custom_call" | custom-call | tf_op jit(solution)/shard_map/loss/pallas_call | solution.py:247
  (8 shorter events, 0.2 us)
Async XLA Ops:
  0.6 42.7 %collective-permute-start.6 = (bf16[7168,256]{1,0:T(8,128)(2,1)}, bf16[7168,256]{1,0:T(8,128)(2,1)S(1)}, u32[]{:S(2)}, u32[]{:S(2)}) collective-permute-start(bf16[7168,256]{1,0:T(8,128)(2,1)} %own.5), channel_id=1, source_target_pairs={{0,1},{1,0},{2,3},{3,2},{4,5},{5,4},{6,7},{7,6},{8,9},{9,8},{10,11... | collective-permute-start | bytes 11010056 | tf_op jit(solution)/shard_map/ppermute | solution.py:51
  1.2 0.9 %copy-start.1 = (bf16[2,4,7168]{2,1,0:T(4,128)(2,1)S(1)}, bf16[2,4,7168]{2,1,0:T(4,128)(2,1)}, u32[]{:S(2)}) copy-start(bf16[2,4,7168]{2,1,0:T(4,128)(2,1)} %hidden.1) | copy-start | bytes 344068
  2.1 5.8 %collective-permute-start = (bf16[8,4736]{1,0:T(8,128)(2,1)S(1)}, bf16[8,4736]{1,0:T(8,128)(2,1)S(1)}, u32[]{:S(2)}, u32[]{:S(2)}) collective-permute-start(bf16[8,4736]{1,0:T(8,128)(2,1)S(1)} %get-tuple-element.8.kept), channel_id=1, source_target_pairs={{0,17},{1,8},{2,11},{3,18},{4,13},{5,20},{6,23},{7,14},{8,1},{9,24... | collective-permute-start | bytes 227336 | tf_op jit(solution)/shard_map/ppermute | solution.py:46
  8.0 6.2 %collective-permute-start.1 = (bf16[16,4736]{1,0:T(8,128)(2,1)S(1)}, bf16[16,4736]{1,0:T(8,128)(2,1)S(1)}, u32[]{:S(2)}, u32[]{:S(2)}) collective-permute-start(bf16[16,4736]{1,0:T(8,128)(2,1)S(1)} %join.6.kept), channel_id=1, source_target_pairs={{0,9},{1,16},{2,19},{3,10},{4,21},{5,12},{6,15},{7,22},{8,25},{9,0... | collective-permute-start | bytes 454664 | tf_op jit(solution)/shard_map/ppermute | solution.py:46
  14.2 6.3 %collective-permute-start.2 = (bf16[32,4736]{1,0:T(8,128)(2,1)S(1)}, bf16[32,4736]{1,0:T(8,128)(2,1)S(1)}, u32[]{:S(2)}, u32[]{:S(2)}) collective-permute-start(bf16[32,4736]{1,0:T(8,128)(2,1)S(1)} %join.7.kept), channel_id=1, source_target_pairs={{0,5},{1,2},{2,1},{3,6},{4,7},{5,0},{6,3},{7,4},{8,11},{9,12},{10,... | collective-permute-start | bytes 909320 | tf_op jit(solution)/shard_map/ppermute | solution.py:46
  20.5 24.5 %collective-permute-start.8 = (bf16[64,4736]{1,0:T(8,128)(2,1)S(1)}, bf16[64,4736]{1,0:T(8,128)(2,1)S(1)}, u32[]{:S(2)}, u32[]{:S(2)}) collective-permute-start(bf16[64,4736]{1,0:T(8,128)(2,1)S(1)} %join.8.kept_a), channel_id=1, source_target_pairs={{0,3},{1,4},{2,7},{3,0},{4,1},{5,6},{6,5},{7,2},{8,13},{9,10},{10,... | collective-permute-start | bytes 1818632 | tf_op jit(solution)/shard_map/ppermute | solution.py:46
  22.0 8.5 %collective-permute-start.3 = (bf16[8,2432]{1,0:T(8,128)(2,1)S(1)}, bf16[8,2432]{1,0:T(8,128)(2,1)S(1)}, u32[]{:S(2)}, u32[]{:S(2)}) collective-permute-start(bf16[8,2432]{1,0:T(8,128)(2,1)S(1)} %get-tuple-element.9.kept), channel_id=1, source_target_pairs={{0,3},{1,4},{2,7},{3,0},{4,1},{5,6},{6,5},{7,2},{8,13},{9,10},{10,... | collective-permute-start | bytes 116744 | tf_op jit(solution)/shard_map/ppermute | solution.py:46
  30.5 4.0 %collective-permute-start.4 = (bf16[16,2432]{1,0:T(8,128)(2,1)S(1)}, bf16[16,2432]{1,0:T(8,128)(2,1)S(1)}, u32[]{:S(2)}, u32[]{:S(2)}) collective-permute-start(bf16[16,2432]{1,0:T(8,128)(2,1)S(1)} %join.9.kept), channel_id=1, source_target_pairs={{0,5},{1,2},{2,1},{3,6},{4,7},{5,0},{6,3},{7,4},{8,11},{9,12},{10,... | collective-permute-start | bytes 233480 | tf_op jit(solution)/shard_map/ppermute | solution.py:46
  34.5 5.3 %collective-permute-start.5 = (bf16[32,2432]{1,0:T(8,128)(2,1)S(1)}, bf16[32,2432]{1,0:T(8,128)(2,1)S(1)}, u32[]{:S(2)}, u32[]{:S(2)}) collective-permute-start(bf16[32,2432]{1,0:T(8,128)(2,1)S(1)} %join.10.kept), channel_id=1, source_target_pairs={{0,9},{1,16},{2,19},{3,10},{4,21},{5,12},{6,15},{7,22},{8,25},{9,0... | collective-permute-start | bytes 466952 | tf_op jit(solution)/shard_map/ppermute | solution.py:46
  39.9 3.7 %copy-start = (bf16[7168,256]{1,0:T(8,128)(2,1)S(1)}, bf16[7168,256]{1,0:T(8,128)(2,1)}, u32[]{:S(2)}) copy-start(bf16[7168,256]{1,0:T(8,128)(2,1)} %own.5) | copy-start | bytes 11010052
  39.9 3.7 %copy-start.2 = (s32[2,128]{1,0:T(2,128)S(1)}, s32[2,128]{1,0:T(2,128)}, u32[]{:S(2)}) copy-start(s32[2,128]{1,0:T(2,128)} %targets.1) | copy-start | bytes 3076
  39.9 10.6 %collective-permute-start.7 = (bf16[64,2432]{1,0:T(8,128)(2,1)S(1)}, bf16[64,2432]{1,0:T(8,128)(2,1)S(1)}, u32[]{:S(2)}, u32[]{:S(2)}) collective-permute-start(bf16[64,2432]{1,0:T(8,128)(2,1)S(1)} %join.11.kept_b), channel_id=1, source_target_pairs={{0,17},{1,8},{2,11},{3,18},{4,13},{5,20},{6,23},{7,14},{8,1},{9,24... | collective-permute-start | bytes 933896 | tf_op jit(solution)/shard_map/ppermute | solution.py:46
  51.3 1.4 %collective-permute-start.9 = (f32[2,128]{1,0:T(2,128)S(1)}, f32[2,128]{1,0:T(2,128)S(1)}, u32[]{:S(2)}, u32[]{:S(2)}) collective-permute-start(f32[2,128]{1,0:T(2,128)S(1)} %stats.1.own), channel_id=1, source_target_pairs={{0,1},{1,0},{2,3},{3,2},{4,5},{5,4},{6,7},{7,6},{8,9},{9,8},{10,11... | collective-permute-start | bytes 3080 | tf_op jit(solution)/shard_map/ppermute | solution.py:51
